TPU v7x, 8 devices: a whole 2x2x1 slice. The times are simulated.
8 devices in a mesh: dp: 2 (over z, y), tp: 4 (over x, core).
Axes of the slice: x: 2, y: 2, z: 1, core: 2. Of those that a mesh axis runs over, the one named last changes fastest.
Arguments:
- hidden: bfloat16 [32, 896], P('dp'), parts along dimension 0
- final_gain: bfloat16 [896], replicated
- embed_table: bfloat16 [151936, 896], P(None, 'tp')
- targets: int32 [32], P('dp'), parts along dimension 0
- temperature: float32 [], replicated
Outputs:
- output 1: float32 [32], P('dp'), parts along dimension 0
- output 2: float32 [32], P('dp'), parts along dimension 0
- output 3: bfloat16 [32, 151936], P('dp', 'tp'), parts along dimension 0
There are 2 independent parts. A program takes and returns all parts, laid end to end along the dimension named above; an argument that names none is the same for every part.
All inputs are finite; a program needn't handle non-finite values.
Results may differ from a plain program's by a relative error of at most 0.0011657.
Values sent between devices are 32-bit elements.
A program may use at most 1 GiB of HBM per device.

v0:
```python
import jax
import jax.numpy as jnp
from jax import lax
from jax.sharding import PartitionSpec as P

NORM_EPS = 1e-6


def solution(mesh):
    def local_scores(hidden, final_gain, table_cols, targets, value_a11):
        shard_index = lax.axis_index('tp')
        col_width = table_cols.shape[1]
        col_start = shard_index * col_width
        hidden_f32 = hidden.astype(jnp.float32)
        inv_rms = lax.rsqrt(jnp.mean(hidden_f32 * hidden_f32, axis=-1, keepdims=True) + NORM_EPS)
        hidden_cols = lax.dynamic_slice_in_dim(hidden, col_start, col_width, axis=1).astype(jnp.float32)
        gain_cols = lax.dynamic_slice_in_dim(final_gain, col_start, col_width).astype(jnp.float32)
        normed_cols = (hidden_cols * inv_rms * gain_cols).astype(jnp.bfloat16)
        partial_logits = lax.dot_general(normed_cols, table_cols, (((1,), (1,)), ((), ())),
                                         preferred_element_type=jnp.float32)
        logits = lax.psum_scatter(partial_logits, 'tp', scatter_dimension=1, tiled=True) / value_a11
        row_max = lax.pmax(jnp.max(logits, axis=-1), 'tp')
        shard_sum = jnp.sum(jnp.exp(logits - row_max[:, None]), axis=-1)
        log_norm = row_max + jnp.log(lax.psum(shard_sum, 'tp'))
        target_rows = jnp.take(table_cols, targets, axis=0)
        target_part = jnp.einsum('nd,nd->n', normed_cols, target_rows,
                                 preferred_element_type=jnp.float32)
        target_logit = lax.psum(target_part, 'tp') / value_a11
        token_probs = jnp.exp(logits - log_norm[:, None]).astype(jnp.bfloat16)
        return log_norm, target_logit - log_norm, token_probs

    return jax.shard_map(local_scores, mesh=mesh,
                         in_specs=(P('dp', None), P(None), P(None, 'tp'), P('dp'), P()),
                         out_specs=(P('dp'), P('dp'), P('dp', 'tp')),
                         check_vma=False)
```

profile of v0, /device:TPU:0, one launch (start us, length us, event | category | flops | bytes accessed | tf_op | source)
XLA Modules:
  0.0 236.0 jit_solution(15671637476082737729)
XLA Ops:
  7.2 0.0 all-reduce.4.cloned.1.call-start
  7.2 0.9 multiply_reduce_fusion
  8.1 0.8 dynamic-slice_convert_fusion
  8.9 27.9 %fusion.1 = f32[16,151936]{1,0:T(8,128)} fusion(bf16[151936,224]{0,1:T(8,128)(2,1)} %param.7, f32[224]{0:T(256)S(1)} %dynamic-slice_convert_fusion, f32[16]{0:T(128)S(1)} %add_rsqrt_fusion, bf16[16,896]{1,0:T(8,128)(2,1)} %param.5, s32[]{:T(128)S(6)} %select_n.13), kind=kOutput, calls=%fused_computation.15 | convolution fusion | flops 1089091584 | bytes 77800384 | tf_op jit(solution)/shard_map/dot_general | solution.py:19
  36.7 0.0 all-reduce.4.cloned.1.call-update
  36.7 0.0 copy-start.2
  36.8 0.0 copy-start.1
  36.8 86.7 %copy.9 = bf16[151936,224]{1,0:T(8,128)(2,1)} copy(bf16[151936,224]{0,1:T(8,128)(2,1)} %param.7) | data formatting | bytes 136134656 | tf_op args[2]
  124.2 0.0 copy-done.2
  124.2 0.6 dynamic-slice
  125.4 0.0 copy-done.1
  125.4 1.3 gather_fusion
  126.7 0.9 fusion
  127.6 81.2 %all-reduce.4.cloned.1.call-done = f32[16,151936]{1,0:T(8,128)} async-done(((f32[16,151936]{1,0:T(8,128)}), f32[16,151936]{1,0:T(8,128)}) %all-reduce.4.cloned.1.call-update) | async-done | bytes 9723920
  208.8 2.5 %fusion.3 = f32[16]{0:T(128)S(1)} fusion(f32[]{:T(128)S(6)} %copy.18, f32[16,151936]{1,0:T(8,128)} %all-reduce.4.cloned.1.call-done, u32[]{:T(128)S(6)} %multiply.8), kind=kLoop, calls=%fused_computation.17 | loop fusion | flops 1215472 | bytes 2431048 | tf_op jit(solution)/shard_map/reduce_max | solution.py:22
  211.3 5.8 %pmax.7 = f32[16]{0:T(128)S(1)} all-reduce(f32[16]{0:T(128)S(1)} %fusion.3), channel_id=1, replica_groups=mesh['dp'=2,'tp'=4] {'tp'}, use_global_device_ids=true, to_apply=%region_3.0 | all-reduce | flops 16 | bytes 128 | tf_op jit(solution)/shard_map/pmax | solution.py:22
  217.1 2.5 %exponential_reduce_fusion = f32[16]{0:T(128)S(1)} fusion(f32[16]{0:T(128)S(1)} %pmax.7, f32[]{:T(128)S(6)} %copy.18, f32[16,151936]{1,0:T(8,128)} %all-reduce.4.cloned.1.call-done, u32[]{:T(128)S(6)} %multiply.8), kind=kLoop, calls=%fused_computation.3 | loop fusion | flops 1823216 | bytes 2431112 | tf_op jit(solution)/shard_map/reduce_sum | solution.py:23
  219.6 5.7 %all-reduce.1 = (f32[16]{0:T(128)S(1)}, f32[16]{0:T(128)S(1)}) all-reduce(f32[16]{0:T(128)S(1)} %exponential_reduce_fusion, f32[16]{0:T(128)S(1)} %fusion), channel_id=1, replica_groups=mesh['dp'=2,'tp'=4] {'tp'}, use_global_device_ids=true, to_apply=%region_5.0 | all-reduce | flops 32 | bytes 256 | tf_op jit(solution)/shard_map/psum | solution.py:24
  225.2 0.5 divide_subtract_fusion
  225.8 0.0 copy-start
  225.8 3.4 %exponential_convert_fusion = bf16[16,37984]{1,0:T(8,128)(2,1)} fusion(f32[16]{0:T(128)S(1)} %get-tuple-element.6, f32[]{:T(128)S(6)} %copy.18, f32[16,151936]{1,0:T(8,128)} %all-reduce.4.cloned.1.call-done, u32[]{:T(128)S(6)} %multiply.8), kind=kLoop, calls=%fused_computation.2 | loop fusion | flops 1823232 | bytes 3646536 | tf_op jit(solution)/shard_map/convert_element_type | solution.py:29
  229.2 0.0 copy-done
  (4 shorter events, 0.0 us)
Async XLA Ops:
  7.2 201.7 %all-reduce.4.cloned.1.call-start = ((), (), s32[]{:S(2)}) async-start(), calls=%async_computation | async-start | bytes 19447808
  36.7 87.4 %copy-start.2 = (u32[8]{0:T(128)S(1)}, u32[8]{0:T(128)}, u32[]{:S(2)}) copy-start(u32[8]{0:T(128)} %constant.37) | copy-start | bytes 100
  36.8 88.7 %copy-start.1 = (s32[16]{0:T(128)S(1)}, s32[16]{0:T(128)}, u32[]{:S(2)}) copy-start(s32[16]{0:T(128)} %param.8) | copy-start | bytes 196
  225.8 3.4 %copy-start = (f32[16]{0:T(128)}, f32[16]{0:T(128)S(1)}, u32[]{:S(2)}) copy-start(f32[16]{0:T(128)S(1)} %get-tuple-element.6) | copy-start | bytes 196
Sparse Core Ops, SparseCore 0:
  36.9 171.9 all-reduce.3
where the time goes:
time: 239 us; the launch traced here: 236 us
  local copies, waits for them, and re-layouts  88.6 us (37%)
  waiting for transfers between devices  81.2 us (34%)
  matrix products  27.9 us (12%)
  between operations  15.4 us (6%)
  other arithmetic  11.5 us (5%)
  blocking collectives  11.4 us (5%)
    unnamed x8, local copies, waits for them, and re-layouts  87.3 us
    unnamed x2, waiting for transfers between devices  81.2 us
    dot_general x1, matrix products, local_scores(): lax.dot_general(normed_cols, table_cols, (((1,), (1,)), ((), ())), prefer...  27.9 us
    pmax x1, blocking collectives, local_scores(): row_max = lax.pmax(jnp.max(logits, axis=-1), 'tp')  5.76 us
    psum x1, blocking collectives, local_scores(): log_norm = row_max + jnp.log(lax.psum(shard_sum, 'tp'))  5.67 us
  transfers between devices with their start and end apart: 1, of which 1 were waited for; matrix products, arithmetic and copies ran while one was open for 38% of the time, Pallas kernels for 0%

commit v1 on v0

v1 whole, which is shorter than its diff:
```python
import math

import jax
import jax.numpy as jnp
from jax import lax
from jax.experimental import pallas as pl
from jax.experimental.pallas import tpu as pltpu
from jax.sharding import PartitionSpec as P

NORM_EPS = 1e-6
LANES = 128
LOG2E = math.log2(math.e)
LN2 = math.log(2.0)
NBLK = 11
DEPTH = 4
LAG = 3


def head_kernel(rows, vocab, tp,
                hid_ref, gain_ref, tgt_ref, temp_ref, tab_ref,
                probs_ref, ln_ref, tl_ref,
                win, stg, mine, part, rx, mk, stat_out, stat_in, ubuf,
                win_sem, edge_sem, psend, precv, xsend, xrecv, ssend, srecv):
    me = lax.axis_index('tp')
    chip = me // 2
    core = me % 2
    partner = chip * 2 + (1 - core)
    across = (1 - chip) * 2 + core
    diag = (1 - chip) * 2 + (1 - core)
    shard = vocab // tp
    tokens, width = hid_ref.shape
    chunk = NBLK * LANES
    nch = pl.cdiv(shard, chunk)
    steps = 2 * nch
    last_blk = vocab // LANES - 1

    def copies(g, which):
        far = g < nch
        k = jnp.where(far, g, g - nch)
        there = jnp.where(far, 1 - chip, chip)
        dest = there * 2 + (jnp.where(which == 0, 1 - core, core))
        blk = (dest * shard) // LANES + k * NBLK
        slot = (g % DEPTH) * 2 + which
        main = pltpu.make_async_copy(
            tab_ref.at[:, pl.ds(pl.multiple_of(blk * LANES, LANES), chunk)],
            win.at[slot, :, pl.ds(0, chunk)], win_sem.at[slot])
        edge_blk = jnp.minimum(blk + NBLK, last_blk)
        edge = pltpu.make_async_copy(
            tab_ref.at[:, pl.ds(pl.multiple_of(edge_blk * LANES, LANES), LANES)],
            win.at[slot, :, pl.ds(chunk, LANES)], edge_sem.at[slot])
        return main, edge, dest, slot

    def fetch(g):
        for which in range(2):
            main, edge, _, _ = copies(g, which)
            main.start()
            edge.start()

    for g in range(DEPTH):
        fetch(g)

    barrier = pltpu.get_barrier_semaphore()
    for peer in (partner, across, diag):
        pl.semaphore_signal(barrier, inc=1, device_id={'tp': peer},
                            device_id_type=pl.DeviceIdType.MESH)

    x = hid_ref[...].astype(jnp.float32)
    inv_rms = lax.rsqrt(jnp.mean(x * x, axis=-1, keepdims=True) + NORM_EPS)
    u_all = x * inv_rms * gain_ref[...].astype(jnp.float32)
    u = u_all[:, :rows]
    for t in range(1, tp):
        u = jnp.where(me == t, u_all[:, t * rows:(t + 1) * rows], u)
    ubuf[...] = u.astype(jnp.bfloat16)

    lane = lax.broadcasted_iota(jnp.int32, (tokens, LANES), 1)
    row = lax.broadcasted_iota(jnp.int32, (tokens, LANES), 0)

    pl.semaphore_wait(barrier, 3)

    def to_partner(g):
        return pltpu.make_async_remote_copy(
            src_ref=stg.at[g], dst_ref=part.at[g], send_sem=psend.at[g], recv_sem=precv.at[g],
            device_id={'tp': partner}, device_id_type=pl.DeviceIdType.MESH)

    def to_across(k):
        return pltpu.make_async_remote_copy(
            src_ref=mine.at[k], dst_ref=rx.at[k], send_sem=xsend.at[k], recv_sem=xrecv.at[k],
            device_id={'tp': across}, device_id_type=pl.DeviceIdType.MESH)

    def partial_logits(g, which, out):
        main, edge, dest, slot = copies(g, which)
        main.wait()
        edge.wait()
        shift = (dest * shard) % LANES
        back = LANES - shift
        z = jnp.dot(ubuf[...], win[slot], preferred_element_type=jnp.float32)
        rolled = [pltpu.roll(z[:, b * LANES:(b + 1) * LANES], back, 1) for b in range(NBLK + 1)]
        for b in range(NBLK):
            out[g, :, b * LANES:(b + 1) * LANES] = jnp.where(lane < back, rolled[b], rolled[b + 1])

    def combine(g):
        to_partner(g).wait_recv()
        mine[g] = mine[g] + part[g]

    def step(g, _):
        partial_logits(g, 0, stg)
        to_partner(g).start()
        partial_logits(g, 1, mine)

        @pl.when(g + DEPTH < steps)
        def _():
            fetch(g + DEPTH)

        h = g - LAG

        @pl.when(h >= 0)
        def _():
            combine(h)

        @pl.when(jnp.logical_and(h >= 0, h < nch))
        def _():
            to_across(h).start()
        return 0

    lax.fori_loop(0, steps, step, 0)
    for h in range(steps - LAG, steps):
        combine(h)

    factor = LOG2E / temp_ref[0]
    target = jnp.zeros((tokens, LANES), jnp.int32)
    for i in range(tokens):
        target = jnp.where(row == i, tgt_ref[i], target)
    target = target - me * shard

    def absorb(k, carry):
        m, s, tg = carry
        to_across(k).wait_recv()
        ts = []
        new_m = m
        for b in range(NBLK):
            cols = slice(b * LANES, (b + 1) * LANES)
            t = (mine[nch + k, :, cols] + rx[k, :, cols]) * factor
            at = lane + (k * chunk + b * LANES)
            t = jnp.where(at < shard, t, -jnp.inf)
            tg = tg + jnp.where(at == target, t, 0.0)
            new_m = jnp.maximum(new_m, t)
            ts.append(t)
        s = s * jnp.exp2(m - new_m)
        for b in range(NBLK):
            p = jnp.exp2(ts[b] - new_m)
            s = s + p
            mine[nch + k, :, b * LANES:(b + 1) * LANES] = p
        mk[k] = new_m
        return new_m, s, tg

    zeros = jnp.zeros((tokens, LANES), jnp.float32)
    m, s, tg = lax.fori_loop(0, nch, absorb, (zeros - jnp.inf, zeros, zeros))

    top = jnp.max(m, axis=-1, keepdims=True)
    total = jnp.sum(s * jnp.exp2(m - top), axis=-1, keepdims=True)
    tval = jnp.sum(tg, axis=-1, keepdims=True)
    packed = jnp.where(lane == 0, top, jnp.where(lane == 1, total, tval))
    stat_out[...] = packed
    sends = [pltpu.make_async_remote_copy(
        src_ref=stat_out, dst_ref=stat_in.at[i], send_sem=ssend.at[i], recv_sem=srecv.at[i],
        device_id={'tp': peer}, device_id_type=pl.DeviceIdType.MESH)
        for i, peer in enumerate((across, diag, partner))]
    for send in sends:
        send.start()
    for send in sends:
        send.wait_recv()
    others = [stat_in[i] for i in range(3)]
    tops = [top] + [o[:, 0:1] for o in others]
    sums = [total] + [o[:, 1:2] for o in others]
    tvals = [tval] + [o[:, 2:3] for o in others]
    big = tops[0]
    for o in tops[1:]:
        big = jnp.maximum(big, o)
    whole = sum(a * jnp.exp2(o - big) for a, o in zip(sums, tops))
    log2_norm = big + jnp.log2(whole)
    picked = sum(tvals)
    ln_ref[...] = jnp.broadcast_to(log2_norm * LN2, (tokens, LANES))
    tl_ref[...] = jnp.broadcast_to((picked - log2_norm) * LN2, (tokens, LANES))

    for k in range(nch):
        scale = jnp.exp2(mk[k] - log2_norm)
        for b in range(NBLK):
            lo = k * chunk + b * LANES
            hi = min(lo + LANES, shard)
            p = mine[nch + k, :, b * LANES:(b + 1) * LANES] * scale
            probs_ref[:, lo:hi] = p.astype(jnp.bfloat16)[:, :hi - lo]

    for send in sends:
        send.wait_send()

    def drain(g, _):
        to_partner(g).wait_send()

        @pl.when(g < nch)
        def _():
            to_across(g).wait_send()
        return 0

    lax.fori_loop(0, steps, drain, 0)


def solution(mesh):
    tp = mesh.shape['tp']

    def local_scores(hidden, final_gain, table_cols, targets, temperature):
        tokens, width = hidden.shape
        vocab, rows = table_cols.shape
        shard = vocab // tp
        chunk = NBLK * LANES
        nch = pl.cdiv(shard, chunk)
        f32 = jnp.float32

        def body(*refs):
            head_kernel(rows, vocab, tp, *refs)

        vm = pl.BlockSpec(memory_space=pltpu.VMEM)
        sm = pl.BlockSpec(memory_space=pltpu.SMEM)
        probs, ln, tl = pl.pallas_call(
            body,
            out_shape=(jax.ShapeDtypeStruct((tokens, shard), jnp.bfloat16),
                       jax.ShapeDtypeStruct((tokens, LANES), f32),
                       jax.ShapeDtypeStruct((tokens, LANES), f32)),
            in_specs=[vm, vm, sm, sm, pl.BlockSpec(memory_space=pl.ANY)],
            out_specs=(vm, vm, vm),
            scratch_shapes=[
                pltpu.VMEM((DEPTH * 2, rows, chunk + LANES), jnp.bfloat16),
                pltpu.VMEM((2 * nch, tokens, chunk), f32),
                pltpu.VMEM((2 * nch, tokens, chunk), f32),
                pltpu.VMEM((2 * nch, tokens, chunk), f32),
                pltpu.VMEM((nch, tokens, chunk), f32),
                pltpu.VMEM((nch, tokens, LANES), f32),
                pltpu.VMEM((tokens, LANES), f32),
                pltpu.VMEM((3, tokens, LANES), f32),
                pltpu.VMEM((tokens, rows), jnp.bfloat16),
                pltpu.SemaphoreType.DMA((DEPTH * 2,)),
                pltpu.SemaphoreType.DMA((DEPTH * 2,)),
                pltpu.SemaphoreType.DMA((2 * nch,)),
                pltpu.SemaphoreType.DMA((2 * nch,)),
                pltpu.SemaphoreType.DMA((nch,)),
                pltpu.SemaphoreType.DMA((nch,)),
                pltpu.SemaphoreType.DMA((3,)),
                pltpu.SemaphoreType.DMA((3,)),
            ],
            compiler_params=pltpu.CompilerParams(
                collective_id=0, has_side_effects=True,
                vmem_limit_bytes=60 * 1024 * 1024),
        )(hidden, final_gain.reshape(1, width), targets, temperature.reshape(1), table_cols.T)
        return ln[:, 0], tl[:, 0], probs

    return jax.shard_map(local_scores, mesh=mesh,
                         in_specs=(P('dp', None), P(None), P(None, 'tp'), P('dp'), P()),
                         out_specs=(P('dp'), P('dp'), P('dp', 'tp')),
                         check_vma=False)
```

time: 239 us -> 73.5 us (0.31); the launches traced: 236 us -> 73.2 us
  local copies, waits for them, and re-layouts: 88.6 us -> 4.99 us
  waiting for transfers between devices: 81.2 us -> 0 us
  Pallas kernels: 0 us -> 67 us
  matrix products: 27.9 us -> 0 us
  between operations: 15.4 us -> 1.29 us
  other arithmetic: 11.5 us -> 0 us
  blocking collectives: 11.4 us -> 0 us
    unnamed x8 -> x1, local copies, waits for them, and re-layouts: 87.3 us -> 2.39 us
    unnamed x2 -> x0, waiting for transfers between devices: 81.2 us -> none
    pallas_call x0 -> x1, Pallas kernels: none -> 67 us  [local_scores(): pl.pallas_call(body, out_shape=(jax.ShapeDtypeStruct((tokens, shard), jnp...]
    dot_general x1 -> x0, matrix products: 27.9 us -> none  [local_scores(): lax.dot_general(normed_cols, table_cols, (((1,), (1,)), ((), ())), prefer...]
    pmax x1 -> x0, blocking collectives: 5.76 us -> none  [local_scores(): row_max = lax.pmax(jnp.max(logits, axis=-1), 'tp')]
    psum x1 -> x0, blocking collectives: 5.67 us -> none  [local_scores(): log_norm = row_max + jnp.log(lax.psum(shard_sum, 'tp'))]
    convert_element_type x2 -> x0, other arithmetic: 4.18 us -> none  [the longest x1 3.42 us: local_scores(): token_probs = jnp.exp(logits - log_norm[:, None]).astype(jnp.bfloat16)]
    reduce_sum x2 -> x0, other arithmetic: 3.37 us -> none  [the longest x1 2.5 us: local_scores(): shard_sum = jnp.sum(jnp.exp(logits - row_max[:, None]), axis=-1)]
  transfers between devices with their start and end apart: 1 -> 0, of which waited for: 1 -> 0; matrix products, arithmetic and copies ran while one was open for 38% -> 0% of each run, Pallas kernels for 0% -> 0%
where the time goes in v1:
time: 73.5 us; the launch traced here: 73.2 us
  Pallas kernels  67 us (91%)
  local copies, waits for them, and re-layouts  4.99 us (7%)
  between operations  1.29 us (2%)
    pallas_call x1, Pallas kernels, local_scores(): pl.pallas_call(body, out_shape=(jax.ShapeDtypeStruct((tokens, shard), jnp...  67 us
    unnamed x1, local copies, waits for them, and re-layouts  2.39 us

profile of v1, /device:TPU:0, one launch (start us, length us, event | category | flops | bytes accessed | tf_op | source)
XLA Modules:
  0.0 73.2 jit_solution(4830880332149412247)
XLA Ops:
  1.3 1.3 %reshape.12.refs_1_ = bf16[1,896]{1,0:T(2,128)(2,1)} reshape(bf16[896]{0:T(1024)(128)(2,1)} %param.6) | data formatting | bytes 3584 | tf_op jit(solution)/shard_map/reshape | solution.py:252
  2.5 67.0 %shard_map.76 = (bf16[16,37984]{1,0:T(8,128)(2,1)}, f32[16,128]{1,0:T(8,128)}, f32[16,128]{1,0:T(8,128)}) custom-call(bf16[16,896]{1,0:T(8,128)(2,1)} %refs_0_.1, bf16[1,896]{1,0:T(2,128)(2,1)} %reshape.12.refs_1_, s32[16]{0:T(128)} %refs_2_.1, f32[1]{0:T(128)} %bitcast.2.refs_3_, bf16[224,151936]{1,0:T(8,128)(2,1)} %bitcast.1.refs_4_), custom_call_target="tpu_custom_call" | custom-call | tf_op jit(solution)/shard_map/pallas_call | solution.py:223
  69.5 1.3 %slice_reduce_fusion = (f32[16]{0:T(128)}, f32[16]{0:T(128)}) fusion(f32[16,128]{1,0:T(8,128)} %get-tuple-element.7, f32[16,128]{1,0:T(8,128)} %get-tuple-element.6), kind=kLoop, calls=%fused_computation | loop fusion | bytes 256 | tf_op jit(solution)/shard_map/slice | solution.py:253
  70.9 2.4 %copy.10 = bf16[16,37984]{1,0:T(8,128)(2,1)} copy(bf16[16,37984]{1,0:T(8,128)(2,1)} %get-tuple-element.16) | data formatting | bytes 2430976

commit v2 on v1

--- a/solution.py
+++ b/solution.py
@@ -12,15 +12,16 @@
 LOG2E = math.log2(math.e)
 LN2 = math.log(2.0)
 NBLK = 11
-DEPTH = 4
-LAG = 3
+FINISH_STEPS = 1
+DEPTH = 3
+LAG = 1
 
 
 def head_kernel(rows, vocab, tp,
-                hid_ref, gain_ref, tgt_ref, temp_ref, tab_ref,
-                probs_ref, ln_ref, tl_ref,
-                win, stg, mine, part, rx, mk, stat_out, stat_in, ubuf,
-                win_sem, edge_sem, psend, precv, xsend, xrecv, ssend, srecv):
+                hid_hbm, gain_hbm, tgt_hbm, temp_ref, tab_ref,
+                pexp_ref, peak_ref, stat_ref,
+                win, stg, mine, part, rx, stat_out, stat_in, ubuf,
+                hid_ref, gain_ref, tgt_ref, in_sem, win_sem, edge_sem, psend, precv, xsend, xrecv, ssend, srecv):
     me = lax.axis_index('tp')
     chip = me // 2
     core = me % 2
@@ -28,7 +29,7 @@
     across = (1 - chip) * 2 + core
     diag = (1 - chip) * 2 + (1 - core)
     shard = vocab // tp
-    tokens, width = hid_ref.shape
+    tokens, width = hid_hbm.shape
     chunk = NBLK * LANES
     nch = pl.cdiv(shard, chunk)
     steps = 2 * nch
@@ -56,17 +57,26 @@
             main.start()
             edge.start()
 
-    for g in range(DEPTH):
-        fetch(g)
-
     barrier = pltpu.get_barrier_semaphore()
     for peer in (partner, across, diag):
         pl.semaphore_signal(barrier, inc=1, device_id={'tp': peer},
                             device_id_type=pl.DeviceIdType.MESH)
 
+    small = [pltpu.make_async_copy(src, dst, in_sem.at[i]) for i, (src, dst) in enumerate((
+        (hid_hbm, hid_ref), (gain_hbm, gain_ref), (tgt_hbm, tgt_ref)))]
+    for copy in small[:2]:
+        copy.start()
+    for g in range(DEPTH):
+        fetch(g)
+    for copy in small[2:]:
+        copy.start()
+    for copy in small[:2]:
+        copy.wait()
+
     x = hid_ref[...].astype(jnp.float32)
     inv_rms = lax.rsqrt(jnp.mean(x * x, axis=-1, keepdims=True) + NORM_EPS)
-    u_all = x * inv_rms * gain_ref[...].astype(jnp.float32)
+    gain = jnp.concatenate([gain_ref[i:i + 1] for i in range(width // LANES)], axis=1).astype(jnp.float32)
+    u_all = x * inv_rms * gain
     u = u_all[:, :rows]
     for t in range(1, tp):
         u = jnp.where(me == t, u_all[:, t * rows:(t + 1) * rows], u)
@@ -126,6 +136,8 @@
     for h in range(steps - LAG, steps):
         combine(h)
 
+    for copy in small[2:]:
+        copy.wait()
     factor = LOG2E / temp_ref[0]
     target = jnp.zeros((tokens, LANES), jnp.int32)
     for i in range(tokens):
@@ -149,8 +161,8 @@
         for b in range(NBLK):
             p = jnp.exp2(ts[b] - new_m)
             s = s + p
-            mine[nch + k, :, b * LANES:(b + 1) * LANES] = p
-        mk[k] = new_m
+            pexp_ref[k, :, b * LANES:(b + 1) * LANES] = p
+        peak_ref[k] = new_m
         return new_m, s, tg
 
     zeros = jnp.zeros((tokens, LANES), jnp.float32)
@@ -179,16 +191,7 @@
     whole = sum(a * jnp.exp2(o - big) for a, o in zip(sums, tops))
     log2_norm = big + jnp.log2(whole)
     picked = sum(tvals)
-    ln_ref[...] = jnp.broadcast_to(log2_norm * LN2, (tokens, LANES))
-    tl_ref[...] = jnp.broadcast_to((picked - log2_norm) * LN2, (tokens, LANES))
-
-    for k in range(nch):
-        scale = jnp.exp2(mk[k] - log2_norm)
-        for b in range(NBLK):
-            lo = k * chunk + b * LANES
-            hi = min(lo + LANES, shard)
-            p = mine[nch + k, :, b * LANES:(b + 1) * LANES] * scale
-            probs_ref[:, lo:hi] = p.astype(jnp.bfloat16)[:, :hi - lo]
+    stat_ref[...] = jnp.where(lane == 0, log2_norm, picked)
 
     for send in sends:
         send.wait_send()
@@ -202,6 +205,27 @@
         return 0
 
     lax.fori_loop(0, steps, drain, 0)
+
+
+def finish_kernel(pexp_ref, peak_ref, stat_ref, probs_ref, ln_ref, tl_ref):
+    tokens = stat_ref.shape[0]
+    log2_norm = stat_ref[:, 0:1]
+    picked = stat_ref[:, 1:2]
+    group = pexp_ref.shape[0] // FINISH_STEPS
+    chunk = pexp_ref.shape[2]
+    first = pl.program_id(0) * group
+    for i in range(group):
+        scale = jnp.exp2(peak_ref[first + i] - log2_norm)
+        for b in range(chunk // LANES):
+            p = pexp_ref[first + i, :, b * LANES:(b + 1) * LANES] * scale
+            probs_ref[:, i * chunk + b * LANES:i * chunk + (b + 1) * LANES] = p.astype(jnp.bfloat16)
+
+    @pl.when(pl.program_id(0) == 0)
+    def _():
+        lane = lax.broadcasted_iota(jnp.int32, (tokens, LANES), 1)
+        row = lax.broadcasted_iota(jnp.int32, (tokens, LANES), 0)
+        for out, val in ((ln_ref, log2_norm * LN2), (tl_ref, (picked - log2_norm) * LN2)):
+            out[...] = jnp.sum(jnp.where(row == lane, val, 0.0), axis=0)[:tokens]
 
 
 def solution(mesh):
@@ -219,13 +243,16 @@
             head_kernel(rows, vocab, tp, *refs)
 
         vm = pl.BlockSpec(memory_space=pltpu.VMEM)
-        sm = pl.BlockSpec(memory_space=pltpu.SMEM)
-        probs, ln, tl = pl.pallas_call(
+        def in_hbm(a):
+            return pltpu.with_memory_space_constraint(a, pltpu.HBM)
+
+        hbm = pl.BlockSpec(memory_space=pltpu.HBM)
+        pexp, peak, stat = pl.pallas_call(
             body,
-            out_shape=(jax.ShapeDtypeStruct((tokens, shard), jnp.bfloat16),
-                       jax.ShapeDtypeStruct((tokens, LANES), f32),
-                       jax.ShapeDtypeStruct((tokens, LANES), f32)),
-            in_specs=[vm, vm, sm, sm, pl.BlockSpec(memory_space=pl.ANY)],
+            out_shape=(pltpu.VMEM((nch, tokens, chunk), f32),
+                       pltpu.VMEM((nch, tokens, LANES), f32),
+                       pltpu.VMEM((tokens, LANES), f32)),
+            in_specs=[hbm, hbm, hbm, pl.BlockSpec(memory_space=pltpu.SMEM), hbm],
             out_specs=(vm, vm, vm),
             scratch_shapes=[
                 pltpu.VMEM((DEPTH * 2, rows, chunk + LANES), jnp.bfloat16),
@@ -233,10 +260,13 @@
                 pltpu.VMEM((2 * nch, tokens, chunk), f32),
                 pltpu.VMEM((2 * nch, tokens, chunk), f32),
                 pltpu.VMEM((nch, tokens, chunk), f32),
-                pltpu.VMEM((nch, tokens, LANES), f32),
                 pltpu.VMEM((tokens, LANES), f32),
                 pltpu.VMEM((3, tokens, LANES), f32),
                 pltpu.VMEM((tokens, rows), jnp.bfloat16),
+                pltpu.VMEM((tokens, width), jnp.bfloat16),
+                pltpu.VMEM((width // LANES, LANES), jnp.bfloat16),
+                pltpu.SMEM((tokens,), jnp.int32),
+                pltpu.SemaphoreType.DMA((3,)),
                 pltpu.SemaphoreType.DMA((DEPTH * 2,)),
                 pltpu.SemaphoreType.DMA((DEPTH * 2,)),
                 pltpu.SemaphoreType.DMA((2 * nch,)),
@@ -248,9 +278,20 @@
             ],
             compiler_params=pltpu.CompilerParams(
                 collective_id=0, has_side_effects=True,
-                vmem_limit_bytes=60 * 1024 * 1024),
-        )(hidden, final_gain.reshape(1, width), targets, temperature.reshape(1), table_cols.T)
-        return ln[:, 0], tl[:, 0], probs
+                vmem_limit_bytes=40 * 1024 * 1024),
+        )(in_hbm(hidden), in_hbm(final_gain.reshape(width // LANES, LANES)), in_hbm(targets),
+          temperature.reshape(1), in_hbm(table_cols.T))
+        keep = [pltpu.with_memory_space_constraint(a, pltpu.VMEM) for a in (pexp, peak, stat)]
+        probs, ln, tl = pl.pallas_call(
+            finish_kernel,
+            grid=(FINISH_STEPS,),
+            out_shape=(pltpu.HBM((tokens, shard), jnp.bfloat16),
+                       pltpu.HBM((tokens,), f32), pltpu.HBM((tokens,), f32)),
+            in_specs=[vm, vm, vm],
+            out_specs=(pl.BlockSpec((tokens, nch // FINISH_STEPS * chunk), lambda i: (0, i)), vm, vm),
+            compiler_params=pltpu.CompilerParams(vmem_limit_bytes=8 * 1024 * 1024),
+        )(*keep)
+        return ln, tl, probs
 
     return jax.shard_map(local_scores, mesh=mesh,
                          in_specs=(P('dp', None), P(None), P(None, 'tp'), P('dp'), P()),

time: 73.5 us -> 66.7 us (0.907)
  local copies, waits for them, and re-layouts: 4.99 us -> 0 us
  Pallas kernels: 67 us -> 65.3 us
    unnamed x1 -> x0, local copies, waits for them, and re-layouts: 2.39 us -> none
    pallas_call x1 -> x2, Pallas kernels: 67 us -> 65.3 us  [the longest x1 64 us: local_scores(): pl.pallas_call(body, out_shape=(pltpu.VMEM((nch, tokens, chunk), f32), pl...]
    slice x1 -> x0, local copies, waits for them, and re-layouts: 1.34 us -> none  [local_scores(): return (ln[:, 0], tl[:, 0], probs)]
    reshape x1 -> x0, local copies, waits for them, and re-layouts: 1.26 us -> none  [local_scores(): final_gain.reshape(1, width)]
where the time goes in v2:
time: 66.7 us; the launch traced here: 66.6 us
  Pallas kernels  65.3 us (98%)
  between operations  1.29 us (2%)
    pallas_call x1, Pallas kernels, local_scores(): pl.pallas_call(body, out_shape=(pltpu.VMEM((nch, tokens, chunk), f32), pl...  64 us

profile of v2, /device:TPU:0, one launch (start us, length us, event | category | flops | bytes accessed | tf_op | source)
XLA Modules:
  0.0 66.6 jit_solution(1490665935099529286)
XLA Ops:
  1.3 64.0 %shard_map.76 = (f32[27,16,1408]{2,1,0:T(8,128)S(1)}, f32[27,16,128]{2,1,0:T(8,128)S(1)}, f32[16,128]{1,0:T(8,128)S(1)}) custom-call(bf16[16,896]{1,0:T(8,128)(2,1)} %refs_0_.1, bf16[7,128]{1,0:T(8,128)(2,1)} %bitcast.4, s32[16]{0:T(128)} %refs_2_.1, f32[1]{0:T(128)} %bitcast.3.refs_3_, bf16[224,151936]{1,0:T(8,128)(2,1)} %bitcast.2.refs_4_), custom_call_target="tpu_custom_call" | custom-call | tf_op jit(solution)/shard_map/pallas_call | solution.py:250
  65.3 1.3 %shard_map.77 = (bf16[16,37984]{1,0:T(8,128)(2,1)}, f32[16]{0:T(128)}, f32[16]{0:T(128)}) custom-call(f32[27,16,1408]{2,1,0:T(8,128)S(1)} %get-tuple-element.9.pexp_ref, f32[27,16,128]{2,1,0:T(8,128)S(1)} %get-tuple-element.10.peak_ref, f32[16,128]{1,0:T(8,128)S(1)} %get-tuple-element.11.stat_ref), custom_call_target="tpu_custom_call" | custom-call | tf_op jit(solution)/shard_map/pallas_call | solution.py:285

commit v3 on v0

v3 whole, which is shorter than its diff:
```python
import math

import jax
import jax.numpy as jnp
from jax import lax
from jax.experimental import pallas as pl
from jax.experimental.pallas import tpu as pltpu
from jax.sharding import PartitionSpec as P

NORM_EPS = 1e-6
LANES = 128
LOG2E = math.log2(math.e)
LN2 = math.log(2.0)
NBLK = 7
TAIL = 3
DEPTH = 3
LAG = 2
RING = 2 * LAG + 2
GROUPS = (1, 1, 2, 4, 6, 8, 8, 6, 4, 2)
PIECES = 6
MESH = pl.DeviceIdType.MESH


def dot(u, window):
    return jnp.dot(u, window, preferred_element_type=jnp.float32)


def head_kernel(rows, vocab, tp,
                hid_hbm, gain_hbm, tgt_hbm, temp_ref, tab_ref,
                pexp_ref, ptail_ref, peak_ref, stat_ref,
                win, twin, stg, mine, part, rx, tout, tin, stat_out, stat_in, ubuf,
                hid_ref, gain_ref, tgt_ref,
                in_sem, win_sem, twin_sem, psend, precv, xsend, xrecv, tsend, trecv, ssend, srecv):
    me = lax.axis_index('tp')
    chip = me // 2
    core = me % 2
    partner = chip * 2 + (1 - core)
    across = (1 - chip) * 2 + core
    diag = (1 - chip) * 2 + (1 - core)
    peers = (across, diag, partner)
    shard = vocab // tp
    tokens, width = hid_hbm.shape
    chunk = NBLK * LANES
    nch = sum(GROUPS)
    steps = 2 * nch
    tail_at = nch * chunk
    last_blk = vocab // LANES - 1

    barrier = pltpu.get_barrier_semaphore()
    for peer in peers:
        pl.semaphore_signal(barrier, inc=1, device_id={'tp': peer}, device_id_type=MESH)

    small = [pltpu.make_async_copy(src, dst, in_sem.at[i]) for i, (src, dst) in enumerate((
        (hid_hbm, hid_ref), (gain_hbm, gain_ref), (tgt_hbm, tgt_ref)))]

    def window(g, which):
        far = g < nch
        k = jnp.where(far, g, g - nch)
        there = jnp.where(far, 1 - chip, chip)
        dest = there * 2 + (jnp.where(which == 0, 1 - core, core))
        blk = (dest * shard) // LANES + k * NBLK
        slot = (g % DEPTH) * 2 + which
        return pltpu.make_async_copy(
            tab_ref.at[:, pl.ds(pl.multiple_of(blk * LANES, LANES), chunk + LANES)],
            win.at[slot], win_sem.at[slot]), dest, slot

    def fetch(g):
        window(g, 0)[0].start()
        window(g, 1)[0].start()

    def tail_window(i, dest):
        blk = (dest * shard) // LANES + nch * NBLK
        edge = jnp.minimum(blk + TAIL, last_blk)
        for at, first, count in ((blk, 0, TAIL), (edge, TAIL, 1)):
            pltpu.make_async_copy(
                tab_ref.at[:, pl.ds(pl.multiple_of(at * LANES, LANES), count * LANES)],
                twin.at[i, :, pl.ds(first * LANES, count * LANES)], twin_sem.at[i]).start()

    tail_dests = (across, diag, partner, me)
    small[0].start()
    small[1].start()
    tail_window(0, across)
    tail_window(1, diag)
    for g in range(DEPTH):
        fetch(g)
    small[2].start()
    tail_window(2, partner)
    tail_window(3, me)
    small[0].wait()
    small[1].wait()

    x = hid_ref[...].astype(jnp.float32)
    inv_rms = lax.rsqrt(jnp.mean(x * x, axis=-1, keepdims=True) + NORM_EPS)
    gain = jnp.concatenate([gain_ref[i:i + 1] for i in range(width // LANES)], axis=1).astype(jnp.float32)
    u_all = x * inv_rms * gain
    u = u_all[:, :rows]
    for t in range(1, tp):
        u = jnp.where(me == t, u_all[:, t * rows:(t + 1) * rows], u)
    ubuf[...] = u.astype(jnp.bfloat16)

    lane = lax.broadcasted_iota(jnp.int32, (tokens, LANES), 1)
    row = lax.broadcasted_iota(jnp.int32, (tokens, LANES), 0)

    def place(z, dest, blocks, store):
        back = LANES - (dest * shard) % LANES
        rolled = [pltpu.roll(z[:, b * LANES:(b + 1) * LANES], back, 1) for b in range(blocks + 1)]
        for b in range(blocks):
            store(b, jnp.where(lane < back, rolled[b], rolled[b + 1]))

    def tail_logits(i):
        pltpu.make_async_copy(tab_ref.at[:, pl.ds(0, (TAIL + 1) * LANES)], twin.at[i], twin_sem.at[i]).wait()

        def store(b, v):
            tout[i, :, b * LANES:(b + 1) * LANES] = v
        place(dot(ubuf[...], twin[i]), tail_dests[i], TAIL, store)

    def tail_send(i):
        return pltpu.make_async_remote_copy(
            src_ref=tout.at[i], dst_ref=tin.at[i], send_sem=tsend.at[0], recv_sem=trecv.at[0],
            device_id={'tp': tail_dests[i]}, device_id_type=MESH)

    tail_logits(0)
    pl.semaphore_wait(barrier, 3)
    tail_send(0).start()
    tail_logits(1)
    tail_send(1).start()

    def to_partner(g):
        return pltpu.make_async_remote_copy(
            src_ref=stg.at[g], dst_ref=part.at[g], send_sem=psend.at[0], recv_sem=precv.at[g % RING],
            device_id={'tp': partner}, device_id_type=MESH)

    starts = [sum(GROUPS[:i]) for i in range(len(GROUPS))]

    def to_across(i):
        chunks = pl.ds(starts[i], GROUPS[i])
        return pltpu.make_async_remote_copy(
            src_ref=mine.at[chunks], dst_ref=rx.at[chunks], send_sem=xsend.at[0], recv_sem=xrecv.at[i],
            device_id={'tp': across}, device_id_type=MESH)

    def partial_logits(g, which, out):
        copy, dest, slot = window(g, which)
        copy.wait()

        def store(b, v):
            out[g, :, b * LANES:(b + 1) * LANES] = v
        place(dot(ubuf[...], win[slot]), dest, NBLK, store)

    def combine(g):
        to_partner(g).wait_recv()
        mine[g] = mine[g] + part[g]

    def step(g, _):
        partial_logits(g, 0, stg)
        to_partner(g).start()
        partial_logits(g, 1, mine)

        @pl.when(g + DEPTH < steps)
        def _():
            fetch(g + DEPTH)

        h = g - LAG

        @pl.when(h >= 0)
        def _():
            combine(h)

        for i, first in enumerate(starts):
            @pl.when(h == first + GROUPS[i] - 1)
            def _():
                to_across(i).start()
        return 0

    lax.fori_loop(0, steps, step, 0)
    tail_logits(2)
    tail_send(2).start()
    tail_logits(3)
    for h in range(steps - LAG, steps):
        combine(h)

    small[2].wait()
    factor = LOG2E / temp_ref[0]
    target = jnp.zeros((tokens, LANES), jnp.int32)
    for i in range(tokens):
        target = jnp.where(row == i, tgt_ref[i], target)
    target = target - me * shard

    def softmax_step(carry, at, ts, store):
        m, s, tg = carry
        new_m = m
        for b, t in enumerate(ts):
            tg = tg + jnp.where(lane + (at + b * LANES) == target, t, 0.0)
            new_m = jnp.maximum(new_m, t)
        s = s * jnp.exp2(m - new_m)
        for b, t in enumerate(ts):
            p = jnp.exp2(t - new_m)
            s = s + p
            store(b, p)
        return new_m, s, tg

    def absorb(k, carry):
        def store(b, p):
            pexp_ref[k, :, b * LANES:(b + 1) * LANES] = p
        ts = [(mine[nch + k, :, b * LANES:(b + 1) * LANES] + rx[k, :, b * LANES:(b + 1) * LANES]) * factor
              for b in range(NBLK)]
        carry = softmax_step(carry, k * chunk, ts, store)
        peak_ref[k] = carry[0]
        return carry

    def absorb_tail(carry):
        pltpu.make_async_copy(tin, tin, trecv.at[0]).wait()

        def store(b, p):
            ptail_ref[:, b * LANES:(b + 1) * LANES] = p
        ts = []
        for b in range(TAIL):
            cols = slice(b * LANES, (b + 1) * LANES)
            t = ((tout[3, :, cols] + tin[2, :, cols]) + (tin[0, :, cols] + tin[1, :, cols])) * factor
            ts.append(jnp.where(lane + (tail_at + b * LANES) < shard, t, -jnp.inf))
        carry = softmax_step(carry, tail_at, ts, store)
        peak_ref[nch] = carry[0]
        return carry

    zeros = jnp.zeros((tokens, LANES), jnp.float32)
    carry = (zeros - jnp.inf, zeros, zeros)
    for i, first in enumerate(starts):
        to_across(i).wait_recv()
        carry = lax.fori_loop(first, first + GROUPS[i], absorb, carry)
        if i == 0:
            carry = absorb_tail(carry)
    m, s, tg = carry

    top = jnp.max(m, axis=-1, keepdims=True)
    total = jnp.sum(s * jnp.exp2(m - top), axis=-1, keepdims=True)
    tval = jnp.sum(tg, axis=-1, keepdims=True)
    half = tokens // 2
    column = lane[:half]
    packed = jnp.zeros((half, LANES), jnp.float32)
    for i, v in enumerate((top, total, tval)):
        packed = jnp.where(column == 2 * i, v[:half], jnp.where(column == 2 * i + 1, v[half:], packed))
    stat_out[...] = packed
    sends = [pltpu.make_async_remote_copy(
        src_ref=stat_out, dst_ref=stat_in.at[i], send_sem=ssend.at[0], recv_sem=srecv.at[0],
        device_id={'tp': peer}, device_id_type=MESH) for i, peer in enumerate(peers)]
    for send in sends:
        send.start()

    pltpu.make_async_copy(stg, stg, psend.at[0]).wait()
    pltpu.make_async_copy(rx, rx, xsend.at[0]).wait()
    pltpu.make_async_copy(tin, tin, tsend.at[0]).wait()

    pltpu.make_async_copy(stat_in, stat_in, srecv.at[0]).wait()
    got = [packed] + [stat_in[i] for i in range(3)]
    for lo in range(2):
        tops = [v[:, lo:lo + 1] for v in got]
        sums = [v[:, 2 + lo:3 + lo] for v in got]
        tvals = [v[:, 4 + lo:5 + lo] for v in got]
        big = jnp.maximum(jnp.maximum(tops[0], tops[1]), jnp.maximum(tops[2], tops[3]))
        whole = sum(a * jnp.exp2(o - big) for a, o in zip(sums, tops))
        log2_norm = big + jnp.log2(whole)
        stat_ref[lo * half:(lo + 1) * half] = jnp.where(column == 0, log2_norm, sum(tvals))
    pltpu.make_async_copy(stat_in, stat_in, ssend.at[0]).wait()


def finish_kernel(pexp_ref, ptail_ref, peak_ref, stat_ref, probs_hbm, ln_hbm, tl_hbm,
                  buf, ln_buf, tl_buf, sem, vec_sem):
    tokens = stat_ref.shape[0]
    nch, _, chunk = pexp_ref.shape
    shard = buf.shape[1]
    log2_norm = stat_ref[:, 0:1]
    picked = stat_ref[:, 1:2]
    copies = []
    for j in range(PIECES):
        lo, hi = nch * j // PIECES, nch * (j + 1) // PIECES
        for k in range(lo, hi):
            scale = jnp.exp2(peak_ref[k] - log2_norm)
            for b in range(chunk // LANES):
                p = pexp_ref[k, :, b * LANES:(b + 1) * LANES] * scale
                buf[:, k * chunk + b * LANES:k * chunk + (b + 1) * LANES] = p.astype(jnp.bfloat16)
        end = hi * chunk
        if j == PIECES - 1:
            scale = jnp.exp2(peak_ref[nch] - log2_norm)
            for at in range(end, shard, LANES):
                p = (ptail_ref[:, at - end:at - end + LANES] * scale).astype(jnp.bfloat16)
                buf[:, at:min(at + LANES, shard)] = p[:, :min(LANES, shard - at)]
            end = shard
        cols = pl.ds(lo * chunk, end - lo * chunk)
        copies.append(pltpu.make_async_copy(buf.at[:, cols], probs_hbm.at[:, cols], sem.at[j]))
        copies[-1].start()
        if j == 1:
            lane = lax.broadcasted_iota(jnp.int32, (tokens, LANES), 1)
            row = lax.broadcasted_iota(jnp.int32, (tokens, LANES), 0)
            for i, (tmp, out, val) in enumerate(((ln_buf, ln_hbm, log2_norm * LN2),
                                                 (tl_buf, tl_hbm, (picked - log2_norm) * LN2))):
                tmp[...] = jnp.sum(jnp.where(row == lane, val, 0.0), axis=0)[:tokens]
                copies.append(pltpu.make_async_copy(tmp, out, vec_sem.at[i]))
                copies[-1].start()
    for copy in copies:
        copy.wait()


def solution(mesh):
    tp = mesh.shape['tp']

    def local_scores(hidden, final_gain, table_cols, targets, temperature):
        tokens, width = hidden.shape
        vocab, rows = table_cols.shape
        shard = vocab // tp
        chunk = NBLK * LANES
        nch = sum(GROUPS)
        f32, bf16 = jnp.float32, jnp.bfloat16

        def body(*refs):
            head_kernel(rows, vocab, tp, *refs)

        def in_hbm(a):
            return pltpu.with_memory_space_constraint(a, pltpu.HBM)

        def dma(n):
            return pltpu.SemaphoreType.DMA((n,))

        vm = pl.BlockSpec(memory_space=pltpu.VMEM)
        hbm = pl.BlockSpec(memory_space=pltpu.HBM)
        outs = pl.pallas_call(
            body,
            out_shape=(pltpu.VMEM((nch, tokens, chunk), f32),
                       pltpu.VMEM((tokens, TAIL * LANES), f32),
                       pltpu.VMEM((nch + 1, tokens, LANES), f32),
                       pltpu.VMEM((tokens, LANES), f32)),
            in_specs=[hbm, hbm, hbm, pl.BlockSpec(memory_space=pltpu.SMEM), hbm],
            out_specs=(vm, vm, vm, vm),
            scratch_shapes=[
                pltpu.VMEM((DEPTH * 2, rows, chunk + LANES), bf16),
                pltpu.VMEM((4, rows, (TAIL + 1) * LANES), bf16),
                pltpu.VMEM((2 * nch, tokens, chunk), f32),
                pltpu.VMEM((2 * nch, tokens, chunk), f32),
                pltpu.VMEM((2 * nch, tokens, chunk), f32),
                pltpu.VMEM((nch, tokens, chunk), f32),
                pltpu.VMEM((4, tokens, TAIL * LANES), f32),
                pltpu.VMEM((3, tokens, TAIL * LANES), f32),
                pltpu.VMEM((tokens // 2, LANES), f32),
                pltpu.VMEM((3, tokens // 2, LANES), f32),
                pltpu.VMEM((tokens, rows), bf16),
                pltpu.VMEM((tokens, width), bf16),
                pltpu.VMEM((width // LANES, LANES), bf16),
                pltpu.SMEM((tokens,), jnp.int32),
                dma(3), dma(DEPTH * 2), dma(4), dma(1), dma(RING), dma(1), dma(len(GROUPS)),
                dma(1), dma(1), dma(1), dma(1),
            ],
            compiler_params=pltpu.CompilerParams(
                collective_id=0, has_side_effects=True, vmem_limit_bytes=40 * 1024 * 1024),
        )(in_hbm(hidden), in_hbm(final_gain.reshape(width // LANES, LANES)), in_hbm(targets),
          temperature.reshape(1), in_hbm(table_cols.T))
        probs, ln, tl = pl.pallas_call(
            finish_kernel,
            out_shape=(pltpu.HBM((tokens, shard), bf16), pltpu.HBM((tokens,), f32), pltpu.HBM((tokens,), f32)),
            in_specs=[vm, vm, vm, vm],
            out_specs=(hbm, hbm, hbm),
            scratch_shapes=[
                pltpu.VMEM((tokens, shard), bf16), pltpu.VMEM((tokens,), f32), pltpu.VMEM((tokens,), f32),
                dma(PIECES), dma(2),
            ],
            compiler_params=pltpu.CompilerParams(vmem_limit_bytes=8 * 1024 * 1024),
        )(*(pltpu.with_memory_space_constraint(a, pltpu.VMEM) for a in outs))
        return ln, tl, probs

    return jax.shard_map(local_scores, mesh=mesh,
                         in_specs=(P('dp', None), P(None), P(None, 'tp'), P('dp'), P()),
                         out_specs=(P('dp'), P('dp'), P('dp', 'tp')),
                         check_vma=False)
```

time: 239 us -> 64.7 us (0.27); the launches traced: 236 us -> 64.6 us
  local copies, waits for them, and re-layouts: 88.6 us -> 0 us
  waiting for transfers between devices: 81.2 us -> 0 us
  Pallas kernels: 0 us -> 63.3 us
  matrix products: 27.9 us -> 0 us
  between operations: 15.4 us -> 1.29 us
  other arithmetic: 11.5 us -> 0 us
  blocking collectives: 11.4 us -> 0 us
    unnamed x8 -> x0, local copies, waits for them, and re-layouts: 87.3 us -> none
    unnamed x2 -> x0, waiting for transfers between devices: 81.2 us -> none
    pallas_call x0 -> x2, Pallas kernels: none -> 63.3 us  [the longest x1 62.1 us: local_scores(): pl.pallas_call(body, out_shape=(pltpu.VMEM((nch, tokens, chunk), f32), pl...]
    dot_general x1 -> x0, matrix products: 27.9 us -> none  [local_scores(): lax.dot_general(normed_cols, table_cols, (((1,), (1,)), ((), ())), prefer...]
    pmax x1 -> x0, blocking collectives: 5.76 us -> none  [local_scores(): row_max = lax.pmax(jnp.max(logits, axis=-1), 'tp')]
    psum x1 -> x0, blocking collectives: 5.67 us -> none  [local_scores(): log_norm = row_max + jnp.log(lax.psum(shard_sum, 'tp'))]
    convert_element_type x2 -> x0, other arithmetic: 4.18 us -> none  [the longest x1 3.42 us: local_scores(): token_probs = jnp.exp(logits - log_norm[:, None]).astype(jnp.bfloat16)]
    reduce_sum x2 -> x0, other arithmetic: 3.37 us -> none  [the longest x1 2.5 us: local_scores(): shard_sum = jnp.sum(jnp.exp(logits - row_max[:, None]), axis=-1)]
  transfers between devices with their start and end apart: 1 -> 0, of which waited for: 1 -> 0; matrix products, arithmetic and copies ran while one was open for 38% -> 0% of each run, Pallas kernels for 0% -> 0%
where the time goes in v3:
time: 64.7 us; the launch traced here: 64.6 us
  Pallas kernels  63.3 us (98%)
  between operations  1.29 us (2%)
    pallas_call x1, Pallas kernels, local_scores(): pl.pallas_call(body, out_shape=(pltpu.VMEM((nch, tokens, chunk), f32), pl...  62.1 us

profile of v3, /device:TPU:0, one launch (start us, length us, event | category | flops | bytes accessed | tf_op | source)
XLA Modules:
  0.0 64.6 jit_solution(2658107437305972703)
XLA Ops:
  1.3 62.1 %shard_map.76 = (f32[42,16,896]{2,1,0:T(8,128)S(1)}, f32[16,384]{1,0:T(8,128)S(1)}, f32[43,16,128]{2,1,0:T(8,128)S(1)}, f32[16,128]{1,0:T(8,128)S(1)}) custom-call(bf16[16,896]{1,0:T(8,128)(2,1)} %refs_0_.1, bf16[7,128]{1,0:T(8,128)(2,1)} %bitcast.4, s32[16]{0:T(128)} %refs_2_.1, f32[1]{0:T(128)} %bitcast.3.refs_3_, bf16[224,151936]{1,0:T(8,128)(2,1)} %bitcast.2.refs_4_), custom_call_target="tpu_custom_call" | custom-call | tf_op jit(solution)/shard_map/pallas_call | solution.py:324
  63.3 1.2 %shard_map.77 = (bf16[16,37984]{1,0:T(8,128)(2,1)}, f32[16]{0:T(128)}, f32[16]{0:T(128)}) custom-call(f32[42,16,896]{2,1,0:T(8,128)S(1)} %get-tuple-element.10.pexp_ref, f32[16,384]{1,0:T(8,128)S(1)} %get-tuple-element.11.ptail_ref, f32[43,16,128]{2,1,0:T(8,128)S(1)} %get-tuple-element.12.peak_ref, f32[16,128]{1,0:T(8,128)S(1)} %get-tuple-element.13.stat_ref), custom_call_target="tpu_custom_call" | custom-call | tf_op jit(solution)/shard_map/pallas_call | solution.py:354

commit v4 on v3

--- a/solution.py
+++ b/solution.py
@@ -17,6 +17,9 @@
 LAG = 2
 RING = 2 * LAG + 2
 GROUPS = (1, 1, 2, 4, 6, 8, 8, 6, 4, 2)
+FAR = 0
+HELD = 5
+HOLD = 36
 PIECES = 6
 MESH = pl.DeviceIdType.MESH
 
@@ -37,7 +40,6 @@
     partner = chip * 2 + (1 - core)
     across = (1 - chip) * 2 + core
     diag = (1 - chip) * 2 + (1 - core)
-    peers = (across, diag, partner)
     shard = vocab // tp
     tokens, width = hid_hbm.shape
     chunk = NBLK * LANES
@@ -47,7 +49,7 @@
     last_blk = vocab // LANES - 1
 
     barrier = pltpu.get_barrier_semaphore()
-    for peer in peers:
+    for peer in (across, diag, partner):
         pl.semaphore_signal(barrier, inc=1, device_id={'tp': peer}, device_id_type=MESH)
 
     small = [pltpu.make_async_copy(src, dst, in_sem.at[i]) for i, (src, dst) in enumerate((
@@ -166,7 +168,9 @@
             combine(h)
 
         for i, first in enumerate(starts):
-            @pl.when(h == first + GROUPS[i] - 1)
+            ready = first + GROUPS[i] - 1
+
+            @pl.when(h == jnp.where(core == FAR, ready, ready if i < HELD else max(ready, HOLD)))
             def _():
                 to_across(i).start()
         return 0
@@ -230,45 +234,62 @@
             carry = absorb_tail(carry)
     m, s, tg = carry
 
-    top = jnp.max(m, axis=-1, keepdims=True)
-    total = jnp.sum(s * jnp.exp2(m - top), axis=-1, keepdims=True)
-    tval = jnp.sum(tg, axis=-1, keepdims=True)
-    half = tokens // 2
-    column = lane[:half]
-    packed = jnp.zeros((half, LANES), jnp.float32)
-    for i, v in enumerate((top, total, tval)):
-        packed = jnp.where(column == 2 * i, v[:half], jnp.where(column == 2 * i + 1, v[half:], packed))
-    stat_out[...] = packed
-    sends = [pltpu.make_async_remote_copy(
-        src_ref=stat_out, dst_ref=stat_in.at[i], send_sem=ssend.at[0], recv_sem=srecv.at[0],
-        device_id={'tp': peer}, device_id_type=MESH) for i, peer in enumerate(peers)]
-    for send in sends:
-        send.start()
+    def stat_send(i, peer):
+        return pltpu.make_async_remote_copy(
+            src_ref=stat_out, dst_ref=stat_in.at[i], send_sem=ssend.at[i], recv_sem=srecv.at[i],
+            device_id={'tp': peer}, device_id_type=MESH)
+
+    def merge(a, b):
+        big = jnp.maximum(a[0], b[0])
+        return big, a[1] * jnp.exp2(a[0] - big) + b[1] * jnp.exp2(b[0] - big), a[2] + b[2]
+
+    def received(i):
+        stat_send(i, partner).wait_recv()
+        return [stat_in[i, j] for j in range(3)]
+
+    def put(values):
+        for i, v in enumerate(values):
+            stat_out[i] = v
+
+    def conclude(stats):
+        big, total, picked = stats
+        top = jnp.max(big, axis=-1, keepdims=True)
+        total = jnp.sum(total * jnp.exp2(big - top), axis=-1, keepdims=True)
+        picked = jnp.sum(picked, axis=-1, keepdims=True)
+        stat_ref[0] = jnp.broadcast_to(top + jnp.log2(total), (tokens, LANES))
+        stat_ref[1] = jnp.broadcast_to(picked, (tokens, LANES))
+
+    @pl.when(core == FAR)
+    def _():
+        put((m, s, tg))
+        stat_send(2, partner).start()
+        chip_stat = received(2)
+        conclude(merge(chip_stat, received(0)))
+        stat_send(2, partner).wait_send()
+
+    @pl.when(core != FAR)
+    def _():
+        chip_stat = merge((m, s, tg), received(2))
+        put(chip_stat)
+        stat_send(0, diag).start()
+        stat_send(1, across).start()
+        stat_send(2, partner).start()
+        conclude(merge(chip_stat, received(1)))
+        for i, peer in enumerate((diag, across, partner)):
+            stat_send(i, peer).wait_send()
 
     pltpu.make_async_copy(stg, stg, psend.at[0]).wait()
     pltpu.make_async_copy(rx, rx, xsend.at[0]).wait()
     pltpu.make_async_copy(tin, tin, tsend.at[0]).wait()
 
-    pltpu.make_async_copy(stat_in, stat_in, srecv.at[0]).wait()
-    got = [packed] + [stat_in[i] for i in range(3)]
-    for lo in range(2):
-        tops = [v[:, lo:lo + 1] for v in got]
-        sums = [v[:, 2 + lo:3 + lo] for v in got]
-        tvals = [v[:, 4 + lo:5 + lo] for v in got]
-        big = jnp.maximum(jnp.maximum(tops[0], tops[1]), jnp.maximum(tops[2], tops[3]))
-        whole = sum(a * jnp.exp2(o - big) for a, o in zip(sums, tops))
-        log2_norm = big + jnp.log2(whole)
-        stat_ref[lo * half:(lo + 1) * half] = jnp.where(column == 0, log2_norm, sum(tvals))
-    pltpu.make_async_copy(stat_in, stat_in, ssend.at[0]).wait()
-
 
 def finish_kernel(pexp_ref, ptail_ref, peak_ref, stat_ref, probs_hbm, ln_hbm, tl_hbm,
                   buf, ln_buf, tl_buf, sem, vec_sem):
-    tokens = stat_ref.shape[0]
+    tokens = stat_ref.shape[1]
     nch, _, chunk = pexp_ref.shape
     shard = buf.shape[1]
-    log2_norm = stat_ref[:, 0:1]
-    picked = stat_ref[:, 1:2]
+    log2_norm = stat_ref[0]
+    picked = stat_ref[1]
     copies = []
     for j in range(PIECES):
         lo, hi = nch * j // PIECES, nch * (j + 1) // PIECES
@@ -326,7 +347,7 @@
             out_shape=(pltpu.VMEM((nch, tokens, chunk), f32),
                        pltpu.VMEM((tokens, TAIL * LANES), f32),
                        pltpu.VMEM((nch + 1, tokens, LANES), f32),
-                       pltpu.VMEM((tokens, LANES), f32)),
+                       pltpu.VMEM((2, tokens, LANES), f32)),
             in_specs=[hbm, hbm, hbm, pl.BlockSpec(memory_space=pltpu.SMEM), hbm],
             out_specs=(vm, vm, vm, vm),
             scratch_shapes=[
@@ -338,14 +359,14 @@
                 pltpu.VMEM((nch, tokens, chunk), f32),
                 pltpu.VMEM((4, tokens, TAIL * LANES), f32),
                 pltpu.VMEM((3, tokens, TAIL * LANES), f32),
-                pltpu.VMEM((tokens // 2, LANES), f32),
-                pltpu.VMEM((3, tokens // 2, LANES), f32),
+                pltpu.VMEM((3, tokens, LANES), f32),
+                pltpu.VMEM((3, 3, tokens, LANES), f32),
                 pltpu.VMEM((tokens, rows), bf16),
                 pltpu.VMEM((tokens, width), bf16),
                 pltpu.VMEM((width // LANES, LANES), bf16),
                 pltpu.SMEM((tokens,), jnp.int32),
                 dma(3), dma(DEPTH * 2), dma(4), dma(1), dma(RING), dma(1), dma(len(GROUPS)),
-                dma(1), dma(1), dma(1), dma(1),
+                dma(1), dma(1), dma(3), dma(3),
             ],
             compiler_params=pltpu.CompilerParams(
                 collective_id=0, has_side_effects=True, vmem_limit_bytes=40 * 1024 * 1024),

time: 64.7 us -> 63.8 us (0.986)
  Pallas kernels: 63.3 us -> 62.4 us
    pallas_call x1, Pallas kernels: 62.1 us -> 61.3 us  [local_scores(): pl.pallas_call(body, out_shape=(pltpu.VMEM((nch, tokens, chunk), f32), pl...]
where the time goes in v4:
time: 63.8 us; the launch traced here: 63.7 us
  Pallas kernels  62.4 us (98%)
  between operations  1.29 us (2%)
    pallas_call x1, Pallas kernels, local_scores(): pl.pallas_call(body, out_shape=(pltpu.VMEM((nch, tokens, chunk), f32), pl...  61.3 us

profile of v4, /device:TPU:0, one launch (start us, length us, event | category | flops | bytes accessed | tf_op | source)
XLA Modules:
  0.0 63.7 jit_solution(15092275008210058036)
XLA Ops:
  1.3 61.3 %shard_map.76 = (f32[42,16,896]{2,1,0:T(8,128)S(1)}, f32[16,384]{1,0:T(8,128)S(1)}, f32[43,16,128]{2,1,0:T(8,128)S(1)}, f32[2,16,128]{2,1,0:T(8,128)S(1)}) custom-call(bf16[16,896]{1,0:T(8,128)(2,1)} %refs_0_.1, bf16[7,128]{1,0:T(8,128)(2,1)} %bitcast.4, s32[16]{0:T(128)} %refs_2_.1, f32[1]{0:T(128)} %bitcast.3.refs_3_, bf16[224,151936]{1,0:T(8,128)(2,1)} %bitcast.2.refs_4_), custom_call_target="tpu_custom_call" | custom-call | tf_op jit(solution)/shard_map/pallas_call | solution.py:345
  62.5 1.1 %shard_map.77 = (bf16[16,37984]{1,0:T(8,128)(2,1)}, f32[16]{0:T(128)}, f32[16]{0:T(128)}) custom-call(f32[42,16,896]{2,1,0:T(8,128)S(1)} %get-tuple-element.10.pexp_ref, f32[16,384]{1,0:T(8,128)S(1)} %get-tuple-element.11.ptail_ref, f32[43,16,128]{2,1,0:T(8,128)S(1)} %get-tuple-element.12.peak_ref, f32[2,16,128]{2,1,0:T(8,128)S(1)} %get-tuple-element.13.stat_ref), custom_call_target="tpu_custom_call" | custom-call | tf_op jit(solution)/shard_map/pallas_call | solution.py:375

commit v5 on v4

--- a/solution.py
+++ b/solution.py
@@ -14,9 +14,8 @@
 NBLK = 7
 TAIL = 3
 DEPTH = 3
-LAG = 2
-RING = 2 * LAG + 2
-GROUPS = (1, 1, 2, 4, 6, 8, 8, 6, 4, 2)
+RING = 6
+GROUPS = (1, 1, 2, 4, 6, 8, 8, 8, 3, 1)
 FAR = 0
 HELD = 5
 HOLD = 36
@@ -66,9 +65,8 @@
             tab_ref.at[:, pl.ds(pl.multiple_of(blk * LANES, LANES), chunk + LANES)],
             win.at[slot], win_sem.at[slot]), dest, slot
 
-    def fetch(g):
-        window(g, 0)[0].start()
-        window(g, 1)[0].start()
+    def fetch(g, which):
+        window(g, which)[0].start()
 
     def tail_window(i, dest):
         blk = (dest * shard) // LANES + nch * NBLK
@@ -81,24 +79,22 @@
     tail_dests = (across, diag, partner, me)
     small[0].start()
     small[1].start()
+    fetch(0, 0)
     tail_window(0, across)
     tail_window(1, diag)
-    for g in range(DEPTH):
-        fetch(g)
-    small[2].start()
-    tail_window(2, partner)
-    tail_window(3, me)
+    fetch(0, 1)
     small[0].wait()
     small[1].wait()
 
     x = hid_ref[...].astype(jnp.float32)
     inv_rms = lax.rsqrt(jnp.mean(x * x, axis=-1, keepdims=True) + NORM_EPS)
     gain = jnp.concatenate([gain_ref[i:i + 1] for i in range(width // LANES)], axis=1).astype(jnp.float32)
-    u_all = x * inv_rms * gain
-    u = u_all[:, :rows]
+    own, own_gain = x[:, :rows], gain[:, :rows]
     for t in range(1, tp):
-        u = jnp.where(me == t, u_all[:, t * rows:(t + 1) * rows], u)
-    ubuf[...] = u.astype(jnp.bfloat16)
+        cols = slice(t * rows, (t + 1) * rows)
+        own = jnp.where(me == t, x[:, cols], own)
+        own_gain = jnp.where(me == t, gain[:, cols], own_gain)
+    ubuf[...] = (own * inv_rms * own_gain).astype(jnp.bfloat16)
 
     lane = lax.broadcasted_iota(jnp.int32, (tokens, LANES), 1)
     row = lax.broadcasted_iota(jnp.int32, (tokens, LANES), 0)
@@ -121,12 +117,6 @@
             src_ref=tout.at[i], dst_ref=tin.at[i], send_sem=tsend.at[0], recv_sem=trecv.at[0],
             device_id={'tp': tail_dests[i]}, device_id_type=MESH)
 
-    tail_logits(0)
-    pl.semaphore_wait(barrier, 3)
-    tail_send(0).start()
-    tail_logits(1)
-    tail_send(1).start()
-
     def to_partner(g):
         return pltpu.make_async_remote_copy(
             src_ref=stg.at[g], dst_ref=part.at[g], send_sem=psend.at[0], recv_sem=precv.at[g % RING],
@@ -152,22 +142,56 @@
         to_partner(g).wait_recv()
         mine[g] = mine[g] + part[g]
 
-    def step(g, _):
+    def fetch_next(g, which):
+        @pl.when(g + DEPTH < steps)
+        def _():
+            fetch(g + DEPTH, which)
+
+    def hand_over(g):
         partial_logits(g, 0, stg)
         to_partner(g).start()
+        fetch_next(g, 0)
+
+    def keep(g):
         partial_logits(g, 1, mine)
-
-        @pl.when(g + DEPTH < steps)
+        fetch_next(g, 1)
+
+    partial_logits(0, 0, stg)
+    fetch(1, 0)
+    fetch(1, 1)
+    fetch(2, 0)
+    fetch(2, 1)
+    small[2].start()
+    tail_window(2, partner)
+    tail_window(3, me)
+    tail_logits(0)
+    pl.semaphore_wait(barrier, 3)
+    to_partner(0).start()
+    tail_send(0).start()
+    tail_logits(1)
+    tail_send(1).start()
+    fetch(DEPTH, 0)
+    hand_over(1)
+    keep(0)
+    combine(0)
+    to_across(0).start()
+    hand_over(2)
+    keep(1)
+    combine(1)
+    to_across(1).start()
+
+    def step(g, _):
+        @pl.when(g + 1 < steps)
         def _():
-            fetch(g + DEPTH)
-
-        h = g - LAG
-
-        @pl.when(h >= 0)
+            hand_over(g + 1)
+        keep(g)
+        h = g - 1
+
+        @pl.when(h >= 2)
         def _():
             combine(h)
 
-        for i, first in enumerate(starts):
+        for i, first in enumerate(starts[2:], 2):
             ready = first + GROUPS[i] - 1
 
             @pl.when(h == jnp.where(core == FAR, ready, ready if i < HELD else max(ready, HOLD)))
@@ -175,12 +199,11 @@
                 to_across(i).start()
         return 0
 
-    lax.fori_loop(0, steps, step, 0)
+    lax.fori_loop(2, steps, step, 0)
     tail_logits(2)
     tail_send(2).start()
     tail_logits(3)
-    for h in range(steps - LAG, steps):
-        combine(h)
+    combine(steps - 1)
 
     small[2].wait()
     factor = LOG2E / temp_ref[0]

time: 63.8 us -> 63.1 us (0.989)
  Pallas kernels: 62.4 us -> 61.7 us
    pallas_call x1, Pallas kernels: 61.3 us -> 60.6 us  [local_scores(): pl.pallas_call(body, out_shape=(pltpu.VMEM((nch, tokens, chunk), f32), pl...]
where the time goes in v5:
time: 63.1 us; the launch traced here: 63 us
  Pallas kernels  61.7 us (98%)
  between operations  1.29 us (2%)
    pallas_call x1, Pallas kernels, local_scores(): pl.pallas_call(body, out_shape=(pltpu.VMEM((nch, tokens, chunk), f32), pl...  60.6 us

profile of v5, /device:TPU:0, one launch (start us, length us, event | category | flops | bytes accessed | tf_op | source)
XLA Modules:
  0.0 63.0 jit_solution(7819065605646760481)
XLA Ops:
  1.3 60.6 %shard_map.76 = (f32[42,16,896]{2,1,0:T(8,128)S(1)}, f32[16,384]{1,0:T(8,128)S(1)}, f32[43,16,128]{2,1,0:T(8,128)S(1)}, f32[2,16,128]{2,1,0:T(8,128)S(1)}) custom-call(bf16[16,896]{1,0:T(8,128)(2,1)} %refs_0_.1, bf16[7,128]{1,0:T(8,128)(2,1)} %bitcast.4, s32[16]{0:T(128)} %refs_2_.1, f32[1]{0:T(128)} %bitcast.3.refs_3_, bf16[224,151936]{1,0:T(8,128)(2,1)} %bitcast.2.refs_4_), custom_call_target="tpu_custom_call" | custom-call | tf_op jit(solution)/shard_map/pallas_call | solution.py:368
  61.9 1.1 %shard_map.77 = (bf16[16,37984]{1,0:T(8,128)(2,1)}, f32[16]{0:T(128)}, f32[16]{0:T(128)}) custom-call(f32[42,16,896]{2,1,0:T(8,128)S(1)} %get-tuple-element.10.pexp_ref, f32[16,384]{1,0:T(8,128)S(1)} %get-tuple-element.11.ptail_ref, f32[43,16,128]{2,1,0:T(8,128)S(1)} %get-tuple-element.12.peak_ref, f32[2,16,128]{2,1,0:T(8,128)S(1)} %get-tuple-element.13.stat_ref), custom_call_target="tpu_custom_call" | custom-call | tf_op jit(solution)/shard_map/pallas_call | solution.py:398

commit v6 on v5

--- a/solution.py
+++ b/solution.py
@@ -19,6 +19,7 @@
 FAR = 0
 HELD = 5
 HOLD = 36
+JOINT = (7, 8, 9, 10)
 PIECES = 6
 MESH = pl.DeviceIdType.MESH
 
@@ -30,9 +31,9 @@
 def head_kernel(rows, vocab, tp,
                 hid_hbm, gain_hbm, tgt_hbm, temp_ref, tab_ref,
                 pexp_ref, ptail_ref, peak_ref, stat_ref,
-                win, twin, stg, mine, part, rx, tout, tin, stat_out, stat_in, ubuf,
+                win, twin, stg, mine, part, rx, tout, tin, stat_out, stat_in, stat_all, ubuf,
                 hid_ref, gain_ref, tgt_ref,
-                in_sem, win_sem, twin_sem, psend, precv, xsend, xrecv, tsend, trecv, ssend, srecv):
+                in_sem, win_sem, twin_sem, psend, precv, xsend, xrecv, tsend, trecv, ssend, srecv, go):
     me = lax.axis_index('tp')
     chip = me // 2
     core = me % 2
@@ -48,8 +49,13 @@
     last_blk = vocab // LANES - 1
 
     barrier = pltpu.get_barrier_semaphore()
-    for peer in (across, diag, partner):
+    for peer in (partner, diag):
         pl.semaphore_signal(barrier, inc=1, device_id={'tp': peer}, device_id_type=MESH)
+
+    @pl.when(core != FAR)
+    def _():
+        pl.semaphore_signal(barrier, inc=1, device_id={'tp': across}, device_id_type=MESH)
+
 
     small = [pltpu.make_async_copy(src, dst, in_sem.at[i]) for i, (src, dst) in enumerate((
         (hid_hbm, hid_ref), (gain_hbm, gain_ref), (tgt_hbm, tgt_ref)))]
@@ -74,14 +80,14 @@
         for at, first, count in ((blk, 0, TAIL), (edge, TAIL, 1)):
             pltpu.make_async_copy(
                 tab_ref.at[:, pl.ds(pl.multiple_of(at * LANES, LANES), count * LANES)],
-                twin.at[i, :, pl.ds(first * LANES, count * LANES)], twin_sem.at[i]).start()
-
-    tail_dests = (across, diag, partner, me)
+                twin.at[i % 2, :, pl.ds(first * LANES, count * LANES)], twin_sem.at[i % 2]).start()
+
+    tail_dests = ((1 - chip) * 2 + (1 - FAR), (1 - chip) * 2 + FAR, partner, me)
     small[0].start()
     small[1].start()
     fetch(0, 0)
-    tail_window(0, across)
-    tail_window(1, diag)
+    tail_window(0, tail_dests[0])
+    tail_window(1, tail_dests[1])
     fetch(0, 1)
     small[0].wait()
     small[1].wait()
@@ -106,15 +112,16 @@
             store(b, jnp.where(lane < back, rolled[b], rolled[b + 1]))
 
     def tail_logits(i):
-        pltpu.make_async_copy(tab_ref.at[:, pl.ds(0, (TAIL + 1) * LANES)], twin.at[i], twin_sem.at[i]).wait()
+        pltpu.make_async_copy(tab_ref.at[:, pl.ds(0, (TAIL + 1) * LANES)], twin.at[i % 2], twin_sem.at[i % 2]).wait()
 
         def store(b, v):
             tout[i, :, b * LANES:(b + 1) * LANES] = v
-        place(dot(ubuf[...], twin[i]), tail_dests[i], TAIL, store)
+        place(dot(ubuf[...], twin[i % 2]), tail_dests[i], TAIL, store)
 
     def tail_send(i):
+        slot = 2 if i == 2 else (jnp.where(core == FAR, 1 - i, i))
         return pltpu.make_async_remote_copy(
-            src_ref=tout.at[i], dst_ref=tin.at[i], send_sem=tsend.at[0], recv_sem=trecv.at[0],
+            src_ref=tout.at[i], dst_ref=tin.at[slot], send_sem=tsend.at[0], recv_sem=trecv.at[0],
             device_id={'tp': tail_dests[i]}, device_id_type=MESH)
 
     def to_partner(g):
@@ -124,10 +131,13 @@
 
     starts = [sum(GROUPS[:i]) for i in range(len(GROUPS))]
 
+    def owner(i):
+        return sum(i >= end for end in JOINT[:-1])
+
     def to_across(i):
         chunks = pl.ds(starts[i], GROUPS[i])
         return pltpu.make_async_remote_copy(
-            src_ref=mine.at[chunks], dst_ref=rx.at[chunks], send_sem=xsend.at[0], recv_sem=xrecv.at[i],
+            src_ref=mine.at[chunks], dst_ref=rx.at[chunks], send_sem=xsend.at[0], recv_sem=xrecv.at[owner(i)],
             device_id={'tp': across}, device_id_type=MESH)
 
     def partial_logits(g, which, out):
@@ -162,13 +172,25 @@
     fetch(2, 0)
     fetch(2, 1)
     small[2].start()
-    tail_window(2, partner)
-    tail_window(3, me)
     tail_logits(0)
-    pl.semaphore_wait(barrier, 3)
+
+    @pl.when(core == FAR)
+    def _():
+        pl.semaphore_wait(barrier, 2)
+
+    @pl.when(core != FAR)
+    def _():
+        pl.semaphore_wait(barrier, 3)
+        pl.semaphore_signal(go, inc=1, device_id={'tp': partner}, device_id_type=MESH)
+
     to_partner(0).start()
     tail_send(0).start()
     tail_logits(1)
+
+    @pl.when(core == FAR)
+    def _():
+        pl.semaphore_wait(go, 1)
+
     tail_send(1).start()
     fetch(DEPTH, 0)
     hand_over(1)
@@ -179,6 +201,8 @@
     keep(1)
     combine(1)
     to_across(1).start()
+    tail_window(2, partner)
+    tail_window(3, me)
 
     def step(g, _):
         @pl.when(g + 1 < steps)
@@ -250,56 +274,62 @@
 
     zeros = jnp.zeros((tokens, LANES), jnp.float32)
     carry = (zeros - jnp.inf, zeros, zeros)
-    for i, first in enumerate(starts):
-        to_across(i).wait_recv()
-        carry = lax.fori_loop(first, first + GROUPS[i], absorb, carry)
-        if i == 0:
+    for j, end in enumerate(JOINT):
+        begin = JOINT[j - 1] if j else 0
+        first, count = starts[begin], sum(GROUPS[begin:end])
+        arrived = rx.at[pl.ds(first, count)]
+        pltpu.make_async_copy(arrived, arrived, xrecv.at[j]).wait()
+        carry = lax.fori_loop(first, first + count, absorb, carry)
+        if j == 0:
             carry = absorb_tail(carry)
     m, s, tg = carry
 
     def stat_send(i, peer):
         return pltpu.make_async_remote_copy(
-            src_ref=stat_out, dst_ref=stat_in.at[i], send_sem=ssend.at[i], recv_sem=srecv.at[i],
+            src_ref=stat_out, dst_ref=stat_in.at[i], send_sem=ssend.at[0], recv_sem=srecv.at[i],
             device_id={'tp': peer}, device_id_type=MESH)
 
     def merge(a, b):
         big = jnp.maximum(a[0], b[0])
         return big, a[1] * jnp.exp2(a[0] - big) + b[1] * jnp.exp2(b[0] - big), a[2] + b[2]
 
+    third = LANES // 4
+
     def received(i):
         stat_send(i, partner).wait_recv()
-        return [stat_in[i, j] for j in range(3)]
+        return [jnp.broadcast_to(stat_in[i, :, j * third:j * third + 1], (tokens, LANES)) for j in range(3)]
 
     def put(values):
-        for i, v in enumerate(values):
-            stat_out[i] = v
+        top, total, picked = values
+        stat_out[...] = jnp.where(lane < third, top, jnp.where(lane < 2 * third, total, picked))
 
     def conclude(stats):
         big, total, picked = stats
-        top = jnp.max(big, axis=-1, keepdims=True)
-        total = jnp.sum(total * jnp.exp2(big - top), axis=-1, keepdims=True)
-        picked = jnp.sum(picked, axis=-1, keepdims=True)
-        stat_ref[0] = jnp.broadcast_to(top + jnp.log2(total), (tokens, LANES))
-        stat_ref[1] = jnp.broadcast_to(picked, (tokens, LANES))
+        stat_ref[0] = big + jnp.log2(total)
+        stat_ref[1] = picked
+
+    top = jnp.max(m, axis=-1, keepdims=True)
+    total = jnp.sum(s * jnp.exp2(m - top), axis=-1, keepdims=True)
+    picked = jnp.sum(tg, axis=-1, keepdims=True)
+    own_stat = [jnp.broadcast_to(v, (tokens, LANES)) for v in (top, total, picked)]
 
     @pl.when(core == FAR)
     def _():
-        put((m, s, tg))
-        stat_send(2, partner).start()
-        chip_stat = received(2)
+        put(own_stat)
+        stat_send(1, partner).start()
+        chip_stat = received(1)
         conclude(merge(chip_stat, received(0)))
-        stat_send(2, partner).wait_send()
+        stat_send(1, partner).wait_send()
 
     @pl.when(core != FAR)
     def _():
-        chip_stat = merge((m, s, tg), received(2))
+        chip_stat = merge(own_stat, received(1))
         put(chip_stat)
         stat_send(0, diag).start()
-        stat_send(1, across).start()
-        stat_send(2, partner).start()
-        conclude(merge(chip_stat, received(1)))
-        for i, peer in enumerate((diag, across, partner)):
-            stat_send(i, peer).wait_send()
+        stat_send(0, across).start()
+        stat_send(1, partner).start()
+        conclude(merge(chip_stat, received(0)))
+        pltpu.make_async_copy(stat_all, stat_all, ssend.at[0]).wait()
 
     pltpu.make_async_copy(stg, stg, psend.at[0]).wait()
     pltpu.make_async_copy(rx, rx, xsend.at[0]).wait()
@@ -375,21 +405,22 @@
             out_specs=(vm, vm, vm, vm),
             scratch_shapes=[
                 pltpu.VMEM((DEPTH * 2, rows, chunk + LANES), bf16),
-                pltpu.VMEM((4, rows, (TAIL + 1) * LANES), bf16),
+                pltpu.VMEM((2, rows, (TAIL + 1) * LANES), bf16),
                 pltpu.VMEM((2 * nch, tokens, chunk), f32),
                 pltpu.VMEM((2 * nch, tokens, chunk), f32),
                 pltpu.VMEM((2 * nch, tokens, chunk), f32),
                 pltpu.VMEM((nch, tokens, chunk), f32),
                 pltpu.VMEM((4, tokens, TAIL * LANES), f32),
                 pltpu.VMEM((3, tokens, TAIL * LANES), f32),
+                pltpu.VMEM((tokens, LANES), f32),
+                pltpu.VMEM((2, tokens, LANES), f32),
                 pltpu.VMEM((3, tokens, LANES), f32),
-                pltpu.VMEM((3, 3, tokens, LANES), f32),
                 pltpu.VMEM((tokens, rows), bf16),
                 pltpu.VMEM((tokens, width), bf16),
                 pltpu.VMEM((width // LANES, LANES), bf16),
                 pltpu.SMEM((tokens,), jnp.int32),
-                dma(3), dma(DEPTH * 2), dma(4), dma(1), dma(RING), dma(1), dma(len(GROUPS)),
-                dma(1), dma(1), dma(3), dma(3),
+                dma(3), dma(DEPTH * 2), dma(2), dma(1), dma(RING), dma(1), dma(len(JOINT)),
+                dma(1), dma(1), dma(1), dma(2), pltpu.SemaphoreType.REGULAR,
             ],
             compiler_params=pltpu.CompilerParams(
                 collective_id=0, has_side_effects=True, vmem_limit_bytes=40 * 1024 * 1024),

time: 63.1 us -> 62.9 us (level)
  no operation moved by 1% of the time
where the time goes in v6:
time: 62.9 us; the launch traced here: 62.8 us
  Pallas kernels  61.5 us (98%)
  between operations  1.29 us (2%)
    pallas_call x1, Pallas kernels, local_scores(): pl.pallas_call(body, out_shape=(pltpu.VMEM((nch, tokens, chunk), f32), pl...  60.4 us

profile of v6, /device:TPU:0, one launch (start us, length us, event | category | flops | bytes accessed | tf_op | source)
XLA Modules:
  0.0 62.8 jit_solution(11603616047407580938)
XLA Ops:
  1.3 60.4 %shard_map.76 = (f32[42,16,896]{2,1,0:T(8,128)S(1)}, f32[16,384]{1,0:T(8,128)S(1)}, f32[43,16,128]{2,1,0:T(8,128)S(1)}, f32[2,16,128]{2,1,0:T(8,128)S(1)}) custom-call(bf16[16,896]{1,0:T(8,128)(2,1)} %refs_0_.1, bf16[7,128]{1,0:T(8,128)(2,1)} %bitcast.4, s32[16]{0:T(128)} %refs_2_.1, f32[1]{0:T(128)} %bitcast.3.refs_3_, bf16[224,151936]{1,0:T(8,128)(2,1)} %bitcast.2.refs_4_), custom_call_target="tpu_custom_call" | custom-call | tf_op jit(solution)/shard_map/pallas_call | solution.py:398
  61.7 1.1 %shard_map.77 = (bf16[16,37984]{1,0:T(8,128)(2,1)}, f32[16]{0:T(128)}, f32[16]{0:T(128)}) custom-call(f32[42,16,896]{2,1,0:T(8,128)S(1)} %get-tuple-element.10.pexp_ref, f32[16,384]{1,0:T(8,128)S(1)} %get-tuple-element.11.ptail_ref, f32[43,16,128]{2,1,0:T(8,128)S(1)} %get-tuple-element.12.peak_ref, f32[2,16,128]{2,1,0:T(8,128)S(1)} %get-tuple-element.13.stat_ref), custom_call_target="tpu_custom_call" | custom-call | tf_op jit(solution)/shard_map/pallas_call | solution.py:429

commit v7 on v6

--- a/solution.py
+++ b/solution.py
@@ -1,5 +1,3 @@
-import math
-
 import jax
 import jax.numpy as jnp
 from jax import lax
@@ -9,8 +7,6 @@
 
 NORM_EPS = 1e-6
 LANES = 128
-LOG2E = math.log2(math.e)
-LN2 = math.log(2.0)
 NBLK = 7
 TAIL = 3
 DEPTH = 3
@@ -56,7 +52,6 @@
     def _():
         pl.semaphore_signal(barrier, inc=1, device_id={'tp': across}, device_id_type=MESH)
 
-
     small = [pltpu.make_async_copy(src, dst, in_sem.at[i]) for i, (src, dst) in enumerate((
         (hid_hbm, hid_ref), (gain_hbm, gain_ref), (tgt_hbm, tgt_ref)))]
 
@@ -230,11 +225,12 @@
     combine(steps - 1)
 
     small[2].wait()
-    factor = LOG2E / temp_ref[0]
+    factor = 1.0 / temp_ref[0]
     target = jnp.zeros((tokens, LANES), jnp.int32)
     for i in range(tokens):
         target = jnp.where(row == i, tgt_ref[i], target)
     target = target - me * shard
+    target = jnp.where(target < shard, target, -1)
 
     def softmax_step(carry, at, ts, store):
         m, s, tg = carry
@@ -242,9 +238,9 @@
         for b, t in enumerate(ts):
             tg = tg + jnp.where(lane + (at + b * LANES) == target, t, 0.0)
             new_m = jnp.maximum(new_m, t)
-        s = s * jnp.exp2(m - new_m)
+        s = s * jnp.exp(m - new_m)
         for b, t in enumerate(ts):
-            p = jnp.exp2(t - new_m)
+            p = jnp.exp(t - new_m)
             s = s + p
             store(b, p)
         return new_m, s, tg
@@ -291,25 +287,25 @@
 
     def merge(a, b):
         big = jnp.maximum(a[0], b[0])
-        return big, a[1] * jnp.exp2(a[0] - big) + b[1] * jnp.exp2(b[0] - big), a[2] + b[2]
-
-    third = LANES // 4
+        return big, a[1] * jnp.exp(a[0] - big) + b[1] * jnp.exp(b[0] - big), a[2] + b[2]
+
+    field = LANES // 4
 
     def received(i):
         stat_send(i, partner).wait_recv()
-        return [jnp.broadcast_to(stat_in[i, :, j * third:j * third + 1], (tokens, LANES)) for j in range(3)]
+        return [jnp.broadcast_to(stat_in[i, :, j * field:j * field + 1], (tokens, LANES)) for j in range(3)]
 
     def put(values):
         top, total, picked = values
-        stat_out[...] = jnp.where(lane < third, top, jnp.where(lane < 2 * third, total, picked))
+        stat_out[...] = jnp.where(lane < field, top, jnp.where(lane < 2 * field, total, picked))
 
     def conclude(stats):
         big, total, picked = stats
-        stat_ref[0] = big + jnp.log2(total)
+        stat_ref[0] = big + jnp.log(total)
         stat_ref[1] = picked
 
     top = jnp.max(m, axis=-1, keepdims=True)
-    total = jnp.sum(s * jnp.exp2(m - top), axis=-1, keepdims=True)
+    total = jnp.sum(s * jnp.exp(m - top), axis=-1, keepdims=True)
     picked = jnp.sum(tg, axis=-1, keepdims=True)
     own_stat = [jnp.broadcast_to(v, (tokens, LANES)) for v in (top, total, picked)]
 
@@ -341,19 +337,19 @@
     tokens = stat_ref.shape[1]
     nch, _, chunk = pexp_ref.shape
     shard = buf.shape[1]
-    log2_norm = stat_ref[0]
+    log_norm = stat_ref[0]
     picked = stat_ref[1]
     copies = []
     for j in range(PIECES):
         lo, hi = nch * j // PIECES, nch * (j + 1) // PIECES
         for k in range(lo, hi):
-            scale = jnp.exp2(peak_ref[k] - log2_norm)
+            scale = jnp.exp(peak_ref[k] - log_norm)
             for b in range(chunk // LANES):
                 p = pexp_ref[k, :, b * LANES:(b + 1) * LANES] * scale
                 buf[:, k * chunk + b * LANES:k * chunk + (b + 1) * LANES] = p.astype(jnp.bfloat16)
         end = hi * chunk
         if j == PIECES - 1:
-            scale = jnp.exp2(peak_ref[nch] - log2_norm)
+            scale = jnp.exp(peak_ref[nch] - log_norm)
             for at in range(end, shard, LANES):
                 p = (ptail_ref[:, at - end:at - end + LANES] * scale).astype(jnp.bfloat16)
                 buf[:, at:min(at + LANES, shard)] = p[:, :min(LANES, shard - at)]
@@ -364,8 +360,8 @@
         if j == 1:
             lane = lax.broadcasted_iota(jnp.int32, (tokens, LANES), 1)
             row = lax.broadcasted_iota(jnp.int32, (tokens, LANES), 0)
-            for i, (tmp, out, val) in enumerate(((ln_buf, ln_hbm, log2_norm * LN2),
-                                                 (tl_buf, tl_hbm, (picked - log2_norm) * LN2))):
+            for i, (tmp, out, val) in enumerate(((ln_buf, ln_hbm, log_norm),
+                                                 (tl_buf, tl_hbm, picked - log_norm))):
                 tmp[...] = jnp.sum(jnp.where(row == lane, val, 0.0), axis=0)[:tokens]
                 copies.append(pltpu.make_async_copy(tmp, out, vec_sem.at[i]))
                 copies[-1].start()

time: 62.9 us -> 62.9 us (level)
  no operation moved by 1% of the time
where the time goes in v7:
time: 62.9 us; the launch traced here: 62.8 us
  Pallas kernels  61.5 us (98%)
  between operations  1.29 us (2%)
    pallas_call x1, Pallas kernels, local_scores(): pl.pallas_call(body, out_shape=(pltpu.VMEM((nch, tokens, chunk), f32), pl...  60.4 us

profile of v7, /device:TPU:0, one launch (start us, length us, event | category | flops | bytes accessed | tf_op | source)
XLA Modules:
  0.0 62.8 jit_solution(6068264658658935299)
XLA Ops:
  1.3 60.4 %shard_map.76 = (f32[42,16,896]{2,1,0:T(8,128)S(1)}, f32[16,384]{1,0:T(8,128)S(1)}, f32[43,16,128]{2,1,0:T(8,128)S(1)}, f32[2,16,128]{2,1,0:T(8,128)S(1)}) custom-call(bf16[16,896]{1,0:T(8,128)(2,1)} %refs_0_.1, bf16[7,128]{1,0:T(8,128)(2,1)} %bitcast.4, s32[16]{0:T(128)} %refs_2_.1, f32[1]{0:T(128)} %bitcast.3.refs_3_, bf16[224,151936]{1,0:T(8,128)(2,1)} %bitcast.2.refs_4_), custom_call_target="tpu_custom_call" | custom-call | tf_op jit(solution)/shard_map/pallas_call | solution.py:394
  61.7 1.1 %shard_map.77 = (bf16[16,37984]{1,0:T(8,128)(2,1)}, f32[16]{0:T(128)}, f32[16]{0:T(128)}) custom-call(f32[42,16,896]{2,1,0:T(8,128)S(1)} %get-tuple-element.10.pexp_ref, f32[16,384]{1,0:T(8,128)S(1)} %get-tuple-element.11.ptail_ref, f32[43,16,128]{2,1,0:T(8,128)S(1)} %get-tuple-element.12.peak_ref, f32[2,16,128]{2,1,0:T(8,128)S(1)} %get-tuple-element.13.stat_ref), custom_call_target="tpu_custom_call" | custom-call | tf_op jit(solution)/shard_map/pallas_call | solution.py:425

commit v8 on v7

--- a/solution.py
+++ b/solution.py
@@ -15,7 +15,7 @@
 FAR = 0
 HELD = 5
 HOLD = 36
-JOINT = (7, 8, 9, 10)
+JOINT = (8, 9, 10)
 PIECES = 6
 MESH = pl.DeviceIdType.MESH
 
@@ -268,10 +268,42 @@
         peak_ref[nch] = carry[0]
         return carry
 
+    def stat_send(i, peer):
+        return pltpu.make_async_remote_copy(
+            src_ref=stat_out, dst_ref=stat_in.at[i], send_sem=ssend.at[0], recv_sem=srecv.at[i],
+            device_id={'tp': peer}, device_id_type=MESH)
+
+    def merge(a, b):
+        big = jnp.maximum(a[0], b[0])
+        return big, a[1] * jnp.exp(a[0] - big) + b[1] * jnp.exp(b[0] - big), a[2] + b[2]
+
+    field = LANES // 4
+
+    def received(i):
+        stat_send(i, partner).wait_recv()
+        return [jnp.broadcast_to(stat_in[i, :, j * field:j * field + 1], (tokens, LANES)) for j in range(3)]
+
+    def put(values):
+        top, total, picked = values
+        stat_out[...] = jnp.where(lane < field, top, jnp.where(lane < 2 * field, total, picked))
+
+    def conclude(stats):
+        big, total, picked = stats
+        stat_ref[0] = big + jnp.log(total)
+        stat_ref[1] = picked
+
+    def take_partner(carry):
+        big, total, picked = merge(carry, received(1))
+        only = lane == 0
+        alone = carry[1] * jnp.exp(carry[0] - big)
+        return big, jnp.where(only, total, alone), jnp.where(only, picked, carry[2])
+
     zeros = jnp.zeros((tokens, LANES), jnp.float32)
     carry = (zeros - jnp.inf, zeros, zeros)
     for j, end in enumerate(JOINT):
         begin = JOINT[j - 1] if j else 0
+        if j == len(JOINT) - 1:
+            carry = lax.cond(core == FAR, lambda c: c, take_partner, carry)
         first, count = starts[begin], sum(GROUPS[begin:end])
         arrived = rx.at[pl.ds(first, count)]
         pltpu.make_async_copy(arrived, arrived, xrecv.at[j]).wait()
@@ -280,30 +312,6 @@
             carry = absorb_tail(carry)
     m, s, tg = carry
 
-    def stat_send(i, peer):
-        return pltpu.make_async_remote_copy(
-            src_ref=stat_out, dst_ref=stat_in.at[i], send_sem=ssend.at[0], recv_sem=srecv.at[i],
-            device_id={'tp': peer}, device_id_type=MESH)
-
-    def merge(a, b):
-        big = jnp.maximum(a[0], b[0])
-        return big, a[1] * jnp.exp(a[0] - big) + b[1] * jnp.exp(b[0] - big), a[2] + b[2]
-
-    field = LANES // 4
-
-    def received(i):
-        stat_send(i, partner).wait_recv()
-        return [jnp.broadcast_to(stat_in[i, :, j * field:j * field + 1], (tokens, LANES)) for j in range(3)]
-
-    def put(values):
-        top, total, picked = values
-        stat_out[...] = jnp.where(lane < field, top, jnp.where(lane < 2 * field, total, picked))
-
-    def conclude(stats):
-        big, total, picked = stats
-        stat_ref[0] = big + jnp.log(total)
-        stat_ref[1] = picked
-
     top = jnp.max(m, axis=-1, keepdims=True)
     total = jnp.sum(s * jnp.exp(m - top), axis=-1, keepdims=True)
     picked = jnp.sum(tg, axis=-1, keepdims=True)
@@ -319,7 +327,7 @@
 
     @pl.when(core != FAR)
     def _():
-        chip_stat = merge(own_stat, received(1))
+        chip_stat = own_stat
         put(chip_stat)
         stat_send(0, diag).start()
         stat_send(0, across).start()

time: 62.9 us -> 62.9 us (level)
  no operation moved by 1% of the time
where the time goes in v8:
time: 62.9 us; the launch traced here: 62.7 us
  Pallas kernels  61.4 us (98%)
  between operations  1.29 us (2%)
    pallas_call x1, Pallas kernels, local_scores(): pl.pallas_call(body, out_shape=(pltpu.VMEM((nch, tokens, chunk), f32), pl...  60.3 us

profile of v8, /device:TPU:0, one launch (start us, length us, event | category | flops | bytes accessed | tf_op | source)
XLA Modules:
  0.0 62.7 jit_solution(2279555880865116343)
XLA Ops:
  1.3 60.3 %shard_map.76 = (f32[42,16,896]{2,1,0:T(8,128)S(1)}, f32[16,384]{1,0:T(8,128)S(1)}, f32[43,16,128]{2,1,0:T(8,128)S(1)}, f32[2,16,128]{2,1,0:T(8,128)S(1)}) custom-call(bf16[16,896]{1,0:T(8,128)(2,1)} %refs_0_.1, bf16[7,128]{1,0:T(8,128)(2,1)} %bitcast.4, s32[16]{0:T(128)} %refs_2_.1, f32[1]{0:T(128)} %bitcast.3.refs_3_, bf16[224,151936]{1,0:T(8,128)(2,1)} %bitcast.2.refs_4_), custom_call_target="tpu_custom_call" | custom-call | tf_op jit(solution)/shard_map/pallas_call | solution.py:402
  61.6 1.1 %shard_map.77 = (bf16[16,37984]{1,0:T(8,128)(2,1)}, f32[16]{0:T(128)}, f32[16]{0:T(128)}) custom-call(f32[42,16,896]{2,1,0:T(8,128)S(1)} %get-tuple-element.10.pexp_ref, f32[16,384]{1,0:T(8,128)S(1)} %get-tuple-element.11.ptail_ref, f32[43,16,128]{2,1,0:T(8,128)S(1)} %get-tuple-element.12.peak_ref, f32[2,16,128]{2,1,0:T(8,128)S(1)} %get-tuple-element.13.stat_ref), custom_call_target="tpu_custom_call" | custom-call | tf_op jit(solution)/shard_map/pallas_call | solution.py:433

commit v9 on v8

--- a/solution.py
+++ b/solution.py
@@ -11,11 +11,11 @@
 TAIL = 3
 DEPTH = 3
 RING = 6
-GROUPS = (1, 1, 2, 4, 6, 8, 8, 8, 3, 1)
+GROUPS = (1, 1, 2, 4, 6, 8, 8, 11, 1)
 FAR = 0
 HELD = 5
 HOLD = 36
-JOINT = (8, 9, 10)
+JOINT = (7, 8, 9)
 PIECES = 6
 MESH = pl.DeviceIdType.MESH
 
@@ -52,7 +52,7 @@
     def _():
         pl.semaphore_signal(barrier, inc=1, device_id={'tp': across}, device_id_type=MESH)
 
-    small = [pltpu.make_async_copy(src, dst, in_sem.at[i]) for i, (src, dst) in enumerate((
+    small = [pltpu.make_async_copy(src, dst, in_sem.at[i % 2]) for i, (src, dst) in enumerate((
         (hid_hbm, hid_ref), (gain_hbm, gain_ref), (tgt_hbm, tgt_ref)))]
 
     def window(g, which):
@@ -277,15 +277,21 @@
         big = jnp.maximum(a[0], b[0])
         return big, a[1] * jnp.exp(a[0] - big) + b[1] * jnp.exp(b[0] - big), a[2] + b[2]
 
-    field = LANES // 4
+    field = LANES // 8
+    half = tokens // 2
 
     def received(i):
         stat_send(i, partner).wait_recv()
-        return [jnp.broadcast_to(stat_in[i, :, j * field:j * field + 1], (tokens, LANES)) for j in range(3)]
+        columns = [stat_in[i, :, j * field:j * field + 1] for j in range(6)]
+        wide = [jnp.broadcast_to(c, (half, LANES)) for c in columns]
+        return [jnp.concatenate(wide[2 * j:2 * j + 2], axis=0) for j in range(3)]
 
     def put(values):
-        top, total, picked = values
-        stat_out[...] = jnp.where(lane < field, top, jnp.where(lane < 2 * field, total, picked))
+        tile = values[2][half:]
+        fields = [v[lo:lo + half] for v in values for lo in (0, half)]
+        for j in range(4, -1, -1):
+            tile = jnp.where(lane[:half] < (j + 1) * field, fields[j], tile)
+        stat_out[...] = tile
 
     def conclude(stats):
         big, total, picked = stats
@@ -416,14 +422,14 @@
                 pltpu.VMEM((nch, tokens, chunk), f32),
                 pltpu.VMEM((4, tokens, TAIL * LANES), f32),
                 pltpu.VMEM((3, tokens, TAIL * LANES), f32),
-                pltpu.VMEM((tokens, LANES), f32),
-                pltpu.VMEM((2, tokens, LANES), f32),
-                pltpu.VMEM((3, tokens, LANES), f32),
+                pltpu.VMEM((tokens // 2, LANES), f32),
+                pltpu.VMEM((2, tokens // 2, LANES), f32),
+                pltpu.VMEM((3, tokens // 2, LANES), f32),
                 pltpu.VMEM((tokens, rows), bf16),
                 pltpu.VMEM((tokens, width), bf16),
                 pltpu.VMEM((width // LANES, LANES), bf16),
                 pltpu.SMEM((tokens,), jnp.int32),
-                dma(3), dma(DEPTH * 2), dma(2), dma(1), dma(RING), dma(1), dma(len(JOINT)),
+                dma(2), dma(DEPTH * 2), dma(2), dma(1), dma(RING), dma(1), dma(len(JOINT)),
                 dma(1), dma(1), dma(1), dma(2), pltpu.SemaphoreType.REGULAR,
             ],
             compiler_params=pltpu.CompilerParams(

time: 62.9 us -> 62.8 us (level)
  no operation moved by 1% of the time
where the time goes in v9:
time: 62.8 us; the launch traced here: 62.7 us
  Pallas kernels  61.4 us (98%)
  between operations  1.29 us (2%)
    pallas_call x1, Pallas kernels, local_scores(): pl.pallas_call(body, out_shape=(pltpu.VMEM((nch, tokens, chunk), f32), pl...  60.2 us

profile of v9, /device:TPU:0, one launch (start us, length us, event | category | flops | bytes accessed | tf_op | source)
XLA Modules:
  0.0 62.7 jit_solution(1256903177718709375)
XLA Ops:
  1.3 60.2 %shard_map.76 = (f32[42,16,896]{2,1,0:T(8,128)S(1)}, f32[16,384]{1,0:T(8,128)S(1)}, f32[43,16,128]{2,1,0:T(8,128)S(1)}, f32[2,16,128]{2,1,0:T(8,128)S(1)}) custom-call(bf16[16,896]{1,0:T(8,128)(2,1)} %refs_0_.1, bf16[7,128]{1,0:T(8,128)(2,1)} %bitcast.4, s32[16]{0:T(128)} %refs_2_.1, f32[1]{0:T(128)} %bitcast.3.refs_3_, bf16[224,151936]{1,0:T(8,128)(2,1)} %bitcast.2.refs_4_), custom_call_target="tpu_custom_call" | custom-call | tf_op jit(solution)/shard_map/pallas_call | solution.py:408
  61.5 1.1 %shard_map.77 = (bf16[16,37984]{1,0:T(8,128)(2,1)}, f32[16]{0:T(128)}, f32[16]{0:T(128)}) custom-call(f32[42,16,896]{2,1,0:T(8,128)S(1)} %get-tuple-element.10.pexp_ref, f32[16,384]{1,0:T(8,128)S(1)} %get-tuple-element.11.ptail_ref, f32[43,16,128]{2,1,0:T(8,128)S(1)} %get-tuple-element.12.peak_ref, f32[2,16,128]{2,1,0:T(8,128)S(1)} %get-tuple-element.13.stat_ref), custom_call_target="tpu_custom_call" | custom-call | tf_op jit(solution)/shard_map/pallas_call | solution.py:439

commit v10 on v9

--- a/solution.py
+++ b/solution.py
@@ -16,7 +16,7 @@
 HELD = 5
 HOLD = 36
 JOINT = (7, 8, 9)
-PIECES = 6
+PIECES = (0, 2, 12, 22, 32, 42)
 MESH = pl.DeviceIdType.MESH
 
 
@@ -29,7 +29,7 @@
                 pexp_ref, ptail_ref, peak_ref, stat_ref,
                 win, twin, stg, mine, part, rx, tout, tin, stat_out, stat_in, stat_all, ubuf,
                 hid_ref, gain_ref, tgt_ref,
-                in_sem, win_sem, twin_sem, psend, precv, xsend, xrecv, tsend, trecv, ssend, srecv, go):
+                in_sem, win_sem, twin_sem, psend, precv, xsend, xrecv, tsend, trecv, srecv, go):
     me = lax.axis_index('tp')
     chip = me // 2
     core = me % 2
@@ -270,7 +270,7 @@
 
     def stat_send(i, peer):
         return pltpu.make_async_remote_copy(
-            src_ref=stat_out, dst_ref=stat_in.at[i], send_sem=ssend.at[0], recv_sem=srecv.at[i],
+            src_ref=stat_out, dst_ref=stat_in.at[i], send_sem=psend.at[0], recv_sem=srecv.at[i],
             device_id={'tp': peer}, device_id_type=MESH)
 
     def merge(a, b):
@@ -304,6 +304,7 @@
         alone = carry[1] * jnp.exp(carry[0] - big)
         return big, jnp.where(only, total, alone), jnp.where(only, picked, carry[2])
 
+    pltpu.make_async_copy(stg, stg, psend.at[0]).wait()
     zeros = jnp.zeros((tokens, LANES), jnp.float32)
     carry = (zeros - jnp.inf, zeros, zeros)
     for j, end in enumerate(JOINT):
@@ -313,7 +314,7 @@
         first, count = starts[begin], sum(GROUPS[begin:end])
         arrived = rx.at[pl.ds(first, count)]
         pltpu.make_async_copy(arrived, arrived, xrecv.at[j]).wait()
-        carry = lax.fori_loop(first, first + count, absorb, carry)
+        carry = absorb(first, carry) if count == 1 else lax.fori_loop(first, first + count, absorb, carry)
         if j == 0:
             carry = absorb_tail(carry)
     m, s, tg = carry
@@ -339,9 +340,8 @@
         stat_send(0, across).start()
         stat_send(1, partner).start()
         conclude(merge(chip_stat, received(0)))
-        pltpu.make_async_copy(stat_all, stat_all, ssend.at[0]).wait()
-
-    pltpu.make_async_copy(stg, stg, psend.at[0]).wait()
+        pltpu.make_async_copy(stat_all, stat_all, psend.at[0]).wait()
+
     pltpu.make_async_copy(rx, rx, xsend.at[0]).wait()
     pltpu.make_async_copy(tin, tin, tsend.at[0]).wait()
 
@@ -354,15 +354,15 @@
     log_norm = stat_ref[0]
     picked = stat_ref[1]
     copies = []
-    for j in range(PIECES):
-        lo, hi = nch * j // PIECES, nch * (j + 1) // PIECES
+    for j in range(len(PIECES) - 1):
+        lo, hi = PIECES[j], PIECES[j + 1]
         for k in range(lo, hi):
             scale = jnp.exp(peak_ref[k] - log_norm)
             for b in range(chunk // LANES):
                 p = pexp_ref[k, :, b * LANES:(b + 1) * LANES] * scale
                 buf[:, k * chunk + b * LANES:k * chunk + (b + 1) * LANES] = p.astype(jnp.bfloat16)
         end = hi * chunk
-        if j == PIECES - 1:
+        if j == len(PIECES) - 2:
             scale = jnp.exp(peak_ref[nch] - log_norm)
             for at in range(end, shard, LANES):
                 p = (ptail_ref[:, at - end:at - end + LANES] * scale).astype(jnp.bfloat16)
@@ -371,7 +371,7 @@
         cols = pl.ds(lo * chunk, end - lo * chunk)
         copies.append(pltpu.make_async_copy(buf.at[:, cols], probs_hbm.at[:, cols], sem.at[j]))
         copies[-1].start()
-        if j == 1:
+        if j == 3:
             lane = lax.broadcasted_iota(jnp.int32, (tokens, LANES), 1)
             row = lax.broadcasted_iota(jnp.int32, (tokens, LANES), 0)
             for i, (tmp, out, val) in enumerate(((ln_buf, ln_hbm, log_norm),
@@ -430,7 +430,7 @@
                 pltpu.VMEM((width // LANES, LANES), bf16),
                 pltpu.SMEM((tokens,), jnp.int32),
                 dma(2), dma(DEPTH * 2), dma(2), dma(1), dma(RING), dma(1), dma(len(JOINT)),
-                dma(1), dma(1), dma(1), dma(2), pltpu.SemaphoreType.REGULAR,
+                dma(1), dma(1), dma(2), pltpu.SemaphoreType.REGULAR,
             ],
             compiler_params=pltpu.CompilerParams(
                 collective_id=0, has_side_effects=True, vmem_limit_bytes=40 * 1024 * 1024),
@@ -443,7 +443,7 @@
             out_specs=(hbm, hbm, hbm),
             scratch_shapes=[
                 pltpu.VMEM((tokens, shard), bf16), pltpu.VMEM((tokens,), f32), pltpu.VMEM((tokens,), f32),
-                dma(PIECES), dma(2),
+                dma(len(PIECES) - 1), dma(2),
             ],
             compiler_params=pltpu.CompilerParams(vmem_limit_bytes=8 * 1024 * 1024),
         )(*(pltpu.with_memory_space_constraint(a, pltpu.VMEM) for a in outs))

time: 62.8 us -> 62.8 us (level)
  no operation moved by 1% of the time
where the time goes in v10:
time: 62.8 us; the launch traced here: 62.7 us
  Pallas kernels  61.4 us (98%)
  between operations  1.29 us (2%)
    pallas_call x1, Pallas kernels, local_scores(): pl.pallas_call(body, out_shape=(pltpu.VMEM((nch, tokens, chunk), f32), pl...  60.2 us

profile of v10, /device:TPU:0, one launch (start us, length us, event | category | flops | bytes accessed | tf_op | source)
XLA Modules:
  0.0 62.7 jit_solution(16836513639821188612)
XLA Ops:
  1.3 60.2 %shard_map.76 = (f32[42,16,896]{2,1,0:T(8,128)S(1)}, f32[16,384]{1,0:T(8,128)S(1)}, f32[43,16,128]{2,1,0:T(8,128)S(1)}, f32[2,16,128]{2,1,0:T(8,128)S(1)}) custom-call(bf16[16,896]{1,0:T(8,128)(2,1)} %refs_0_.1, bf16[7,128]{1,0:T(8,128)(2,1)} %bitcast.4, s32[16]{0:T(128)} %refs_2_.1, f32[1]{0:T(128)} %bitcast.3.refs_3_, bf16[224,151936]{1,0:T(8,128)(2,1)} %bitcast.2.refs_4_), custom_call_target="tpu_custom_call" | custom-call | tf_op jit(solution)/shard_map/pallas_call | solution.py:408
  61.5 1.1 %shard_map.77 = (bf16[16,37984]{1,0:T(8,128)(2,1)}, f32[16]{0:T(128)}, f32[16]{0:T(128)}) custom-call(f32[42,16,896]{2,1,0:T(8,128)S(1)} %get-tuple-element.10.pexp_ref, f32[16,384]{1,0:T(8,128)S(1)} %get-tuple-element.11.ptail_ref, f32[43,16,128]{2,1,0:T(8,128)S(1)} %get-tuple-element.12.peak_ref, f32[2,16,128]{2,1,0:T(8,128)S(1)} %get-tuple-element.13.stat_ref), custom_call_target="tpu_custom_call" | custom-call | tf_op jit(solution)/shard_map/pallas_call | solution.py:439

commit v11 on v10

--- a/solution.py
+++ b/solution.py
@@ -45,12 +45,12 @@
     last_blk = vocab // LANES - 1
 
     barrier = pltpu.get_barrier_semaphore()
-    for peer in (partner, diag):
+    @pl.when(core != FAR)
+    def _():
+        pl.semaphore_signal(barrier, inc=1, device_id={'tp': across}, device_id_type=MESH)
+
+    for peer in (diag, partner):
         pl.semaphore_signal(barrier, inc=1, device_id={'tp': peer}, device_id_type=MESH)
-
-    @pl.when(core != FAR)
-    def _():
-        pl.semaphore_signal(barrier, inc=1, device_id={'tp': across}, device_id_type=MESH)
 
     small = [pltpu.make_async_copy(src, dst, in_sem.at[i % 2]) for i, (src, dst) in enumerate((
         (hid_hbm, hid_ref), (gain_hbm, gain_ref), (tgt_hbm, tgt_ref)))]
@@ -270,7 +270,7 @@
 
     def stat_send(i, peer):
         return pltpu.make_async_remote_copy(
-            src_ref=stat_out, dst_ref=stat_in.at[i], send_sem=psend.at[0], recv_sem=srecv.at[i],
+            src_ref=stat_out, dst_ref=stat_in.at[i], send_sem=psend.at[0], recv_sem=precv.at[0] if i else srecv.at[0],
             device_id={'tp': peer}, device_id_type=MESH)
 
     def merge(a, b):
@@ -430,7 +430,7 @@
                 pltpu.VMEM((width // LANES, LANES), bf16),
                 pltpu.SMEM((tokens,), jnp.int32),
                 dma(2), dma(DEPTH * 2), dma(2), dma(1), dma(RING), dma(1), dma(len(JOINT)),
-                dma(1), dma(1), dma(2), pltpu.SemaphoreType.REGULAR,
+                dma(1), dma(1), dma(1), pltpu.SemaphoreType.REGULAR,
             ],
             compiler_params=pltpu.CompilerParams(
                 collective_id=0, has_side_effects=True, vmem_limit_bytes=40 * 1024 * 1024),

time: 62.8 us -> 62.8 us (level)
  no operation moved by 1% of the time
where the time goes in v11:
time: 62.8 us; the launch traced here: 62.7 us
  Pallas kernels  61.4 us (98%)
  between operations  1.29 us (2%)
    pallas_call x1, Pallas kernels, local_scores(): pl.pallas_call(body, out_shape=(pltpu.VMEM((nch, tokens, chunk), f32), pl...  60.2 us

profile of v11, /device:TPU:0, one launch (start us, length us, event | category | flops | bytes accessed | tf_op | source)
XLA Modules:
  0.0 62.7 jit_solution(16223321707342267029)
XLA Ops:
  1.3 60.2 %shard_map.76 = (f32[42,16,896]{2,1,0:T(8,128)S(1)}, f32[16,384]{1,0:T(8,128)S(1)}, f32[43,16,128]{2,1,0:T(8,128)S(1)}, f32[2,16,128]{2,1,0:T(8,128)S(1)}) custom-call(bf16[16,896]{1,0:T(8,128)(2,1)} %refs_0_.1, bf16[7,128]{1,0:T(8,128)(2,1)} %bitcast.4, s32[16]{0:T(128)} %refs_2_.1, f32[1]{0:T(128)} %bitcast.3.refs_3_, bf16[224,151936]{1,0:T(8,128)(2,1)} %bitcast.2.refs_4_), custom_call_target="tpu_custom_call" | custom-call | tf_op jit(solution)/shard_map/pallas_call | solution.py:408
  61.5 1.1 %shard_map.77 = (bf16[16,37984]{1,0:T(8,128)(2,1)}, f32[16]{0:T(128)}, f32[16]{0:T(128)}) custom-call(f32[42,16,896]{2,1,0:T(8,128)S(1)} %get-tuple-element.10.pexp_ref, f32[16,384]{1,0:T(8,128)S(1)} %get-tuple-element.11.ptail_ref, f32[43,16,128]{2,1,0:T(8,128)S(1)} %get-tuple-element.12.peak_ref, f32[2,16,128]{2,1,0:T(8,128)S(1)} %get-tuple-element.13.stat_ref), custom_call_target="tpu_custom_call" | custom-call | tf_op jit(solution)/shard_map/pallas_call | solution.py:439
